TPU v7x, 32 devices: a whole 2x2x4 slice. The times are simulated.
32 devices in a mesh: dp: 8 (over y, x, core), expert: 4 (over z).
Axes of the slice: x: 2, y: 2, z: 4, core: 2. Of those that a mesh axis runs over, the one named last changes fastest.
Arguments:
- inputs: bfloat16 [2, 6304, 384], P(None, ('dp', 'expert')), may hold values from -6 to 6
- first_gain: float32 [384], replicated, may hold values from 0.25 to 1.75
- w_qkv: bfloat16 [384, 1152], replicated, may hold values from -0.3125 to 0.3125
- w_attn: bfloat16 [384, 384], replicated, may hold values from -1.75 to 1.75
- second_gain: float32 [384], replicated, may hold values from 0.25 to 1.75
- w_router: bfloat16 [384, 16], replicated, may hold values from -0.625 to 0.625
- expert_in: bfloat16 [16, 384, 1536], P('expert'), may hold values from -0.3125 to 0.3125
- expert_out: bfloat16 [16, 1536, 384], P('expert'), may hold values from -2.5 to 2.5
- expert_ids: int32 [2, 6304, 2], P(None, ('dp', 'expert')), may hold values from 0 to 15, as said below
- slot_ids: int32 [2, 6304, 2], P(None, ('dp', 'expert')), may hold values from 0 to 15, as said below
- dropped: int32 [2, 6304, 2], P(None, ('dp', 'expert')), may hold values from 0 to 1, as said below
- out_grad: bfloat16 [2, 6304, 384], P(None, ('dp', 'expert')), may hold values from -6 to 6
Outputs:
- block_out: float32 [2, 6304, 384], P(None, ('dp', 'expert'))
- input_grad: float32 [2, 6304, 384], P(None, ('dp', 'expert'))
- first_gain_grad: float32 [384], replicated
- w_qkv_grad: float32 [384, 1152], replicated
- w_attn_grad: float32 [384, 384], replicated
- second_gain_grad: float32 [384], replicated
- w_router_grad: float32 [384, 16], replicated
- expert_in_grad: float32 [16, 384, 1536], P('expert', None, 'dp')
- expert_out_grad: float32 [16, 1536, 384], P('expert', 'dp')
Inputs may be any that keep to these rules, and one draw needn't show every extreme that they name: `expert_ids`: the two experts of a token differ. `slot_ids`: in each micro-batch and each device's block of 197 tokens, the pairs are taken in order (first choices of all tokens in token order, then second choices); a pair gets the number of earlier pairs of the block naming its expert as slot if that is under 16, else it is dropped and has slot 0. `dropped`: 1 exactly where the pair's expert already had 16 pairs of the block before it.
All inputs are finite; a program needn't handle non-finite values.
Results may differ from a plain program's by a relative error of at most 0.015.
The roundings to bfloat16 on the way count: a program that leaves them out, or rounds other values in their place, can miss the bound.
Values may be sent and summed in bfloat16 or wider, within the bound.
A program may use at most 128 MiB of HBM per device.

v0:
```python
import functools

import jax
import jax.numpy as jnp
from jax import lax
from jax.experimental import pallas as pl
from jax.experimental.pallas import tpu as pltpu
from jax.sharding import PartitionSpec as P

D = 384
HEADS = 6
HD = 64
SEQ = 197
MB = 2
CAP = 16
EPS = 1e-06
TP = 208
TL = 256
XR = 16
F32 = jnp.float32
BF16 = jnp.bfloat16
MESH = pl.DeviceIdType.MESH


def mm(a, b, ca=1, cb=0):
    return lax.dot_general(
        a, b, (((ca,), (cb,)), ((), ())), preferred_element_type=F32
    )


def normed_of(rows):
    mean = jnp.sum(rows, axis=-1, keepdims=True) * (1.0 / D)
    centered = rows - mean
    var = jnp.sum(centered * centered, axis=-1, keepdims=True) * (1.0 / D)
    rstd = lax.rsqrt(var + EPS)
    return centered * rstd, rstd


def norm_pull(hat, rstd, gain, grad):
    scaled = grad * gain
    m1 = jnp.sum(scaled, axis=-1, keepdims=True) * (1.0 / D)
    m2 = jnp.sum(scaled * hat, axis=-1, keepdims=True) * (1.0 / D)
    return rstd * (scaled - m1 - hat * m2)


def kernel(
    dims,
    x_ref,
    g_ref,
    gain1_ref,
    gain2_ref,
    wqkv_ref,
    wattn_ref,
    wrt_ref,
    ids_ref,
    slot_ref,
    drop_ref,
    win_hbm,
    wout_hbm,
    bo_ref,
    ig_ref,
    eg_ref,
    ag_ref,
    w1,
    w2,
    n1_ref,
    qkv_ref,
    p_ref,
    am_ref,
    res_ref,
    n2_ref,
    rs_ref,
    cols_ref,
    dsend,
    drecv,
    rsend,
    rrecv,
    act_ref,
    hg_ref,
    xr_ref,
    pr_ref,
    xg_ref,
    x1_ref,
    xs_ref,
    dq_ref,
    acc_ref,
    small_ref,
    arb_ref,
    l1_ref,
    l2s_ref,
    l2_ref,
    l3_ref,
    wsem,
    dsem,
    rsem,
    xsem,
    asem,
):
    L, R, Z, G, FF = dims
    S = G * CAP
    FS = FF // (L * R)
    PR = arb_ref.shape[2]
    NR = PR - XR
    dp = lax.axis_index("dp")
    z = lax.axis_index("expert")
    j = dp // R
    r = dp % R
    me = z * L + j

    def group_id(e):
        return ((e % L) * R + r, e // L)

    def plane_id(i):
        return (i * R + r, z)

    def part_id(rr):
        return (j * R + rr, z)

    def remote(src, dst, sems, device):
        return pltpu.make_async_remote_copy(
            src_ref=src,
            dst_ref=dst,
            send_sem=sems.at[0],
            recv_sem=sems.at[1],
            device_id=device,
            device_id_type=MESH,
        )

    def wait_bytes(ref, sem):
        pltpu.make_async_copy(ref, ref, sem).wait()

    barrier = pltpu.get_barrier_semaphore()

    @pl.loop(1, G)
    def _(o):
        pl.semaphore_signal(
            barrier, inc=1, device_id=group_id((me + o) % G), device_id_type=MESH
        )

    for o in range(1, R):
        pl.semaphore_signal(
            barrier, inc=1, device_id=part_id((r + o) % R), device_id_type=MESH
        )

    load1 = pltpu.make_async_copy(win_hbm.at[j], w1, wsem.at[0])
    load2 = pltpu.make_async_copy(wout_hbm.at[j], w2, wsem.at[1])
    load1.start()
    load2.start()
    pl.semaphore_wait(barrier, G - 1 + R - 1)

    lane128 = lax.broadcasted_iota(jnp.int32, (TP, 128), 1)
    low_half = lane128 < HD
    key_ok = lax.broadcasted_iota(jnp.int32, (TP, TP), 1) < SEQ

    def exchange(send, recv, sems):
        pltpu.make_async_copy(send.at[me], recv.at[me], sems.at[1]).start()

        @pl.loop(1, G)
        def _(o):
            e = (me + o) % G
            remote(send.at[e], recv.at[me], sems, group_id(e)).start()

    def forward(mb, carry):
        x = x_ref[mb].astype(F32)
        hat, _ = normed_of(x)
        n1 = (hat * gain1_ref[...]).astype(BF16)
        n1_ref[mb] = n1
        qkv_ref[mb] = mm(n1, wqkv_ref[...]).astype(BF16)
        for pair in range(HEADS // 2):
            c = pair * 128
            q = qkv_ref[mb, :, c : c + 128] * jnp.asarray(HD**-0.5, BF16)
            k = qkv_ref[mb, :, D + c : D + c + 128]
            v = qkv_ref[mb, :, 2 * D + c : 2 * D + c + 128]
            mixed = []
            for half in range(2):
                mine = low_half if half == 0 else jnp.logical_not(low_half)
                qh = jnp.where(mine, q, jnp.zeros_like(q))
                s = mm(qh, k, 1, 1)
                s = jnp.where(key_ok, s, -1e30)
                e = jnp.exp(s - jnp.max(s, axis=-1, keepdims=True))
                p = e / jnp.sum(e, axis=-1, keepdims=True)
                p_ref[mb, 2 * pair + half] = p
                mixed.append(mm(p.astype(BF16), v))
            am_ref[mb, :, c : c + 128] = jnp.where(
                low_half, mixed[0], mixed[1]
            ).astype(BF16)
        res = x + mm(am_ref[mb], wattn_ref[...])
        res_ref[mb] = res
        hat2, _ = normed_of(res)
        n2 = (hat2 * gain2_ref[...]).astype(BF16)
        n2_ref[mb] = n2
        logits = mm(wrt_ref[...], n2, 1, 1)
        ex = jnp.exp(logits - jnp.max(logits, axis=0, keepdims=True))
        gp = ex / jnp.sum(ex, axis=0, keepdims=True)
        ids = ids_ref[mb]
        drop = drop_ref[mb]
        flat = jnp.where(drop == 0, ids * CAP + slot_ref[mb], S)
        rs_ref[...] = jnp.zeros_like(rs_ref)
        rs_ref[0:G, 0:TP] = gp
        rs_ref[G : G + 2, 0:TP] = jnp.full((2, TP), S, F32)
        rs_ref[G : G + 2, 0:SEQ] = flat.astype(F32)
        rs_ref[G + 2 : G + 4, 0:SEQ] = 1.0 - drop.astype(F32)
        rs_ref[G + 4 : G + 6, 0:SEQ] = ids.astype(F32)
        expert_of = lax.broadcasted_iota(jnp.int32, (G, TP), 0).astype(F32)
        slot_of = lax.broadcasted_iota(jnp.int32, (S, TP), 0).astype(F32)
        picks = []
        gcol = jnp.zeros((S, 1), F32)
        for kk in range(2):
            idr = rs_ref[G + 4 + kk : G + 5 + kk, 0:TP]
            keep = rs_ref[G + 2 + kk : G + 3 + kk, 0:TP]
            flr = rs_ref[G + kk : G + kk + 1, 0:TP]
            gate = (
                jnp.sum(jnp.where(expert_of == idr, gp, 0.0), axis=0, keepdims=True)
                * keep
            )
            rs_ref[G + 6 + kk : G + 7 + kk, 0:TP] = gate
            hit = slot_of == flr
            picks.append(jnp.where(hit, 1.0, 0.0))
            gcol = gcol + jnp.sum(
                jnp.where(hit, gate, 0.0), axis=-1, keepdims=True
            )
        cols_ref[mb] = rs_ref[...].T
        pick = (picks[0] + picks[1]).astype(BF16)
        rows = mm(pick, n2).astype(BF16)
        dsend[mb, :, 0:CAP, :] = rows.reshape(G, CAP, D)
        grows = (mm(pick, g_ref[mb]) * gcol).astype(BF16)
        dsend[mb, :, CAP : 2 * CAP, :] = grows.reshape(G, CAP, D)
        exchange(dsend.at[mb], drecv.at[mb], dsem.at[mb])
        return carry

    lax.fori_loop(0, MB, forward, 0)
    load1.wait()
    load2.wait()

    def experts(mb, carry):
        wait_bytes(drecv.at[mb], dsem.at[mb, 1])
        xs = drecv[mb, :, 0:CAP, :].reshape(S, D)
        pg = drecv[mb, :, CAP : 2 * CAP, :].reshape(S, D)
        base = pl.multiple_of(mb * S, S)
        xr_ref[pl.ds(base, S), :] = xs
        pr_ref[pl.ds(base, S), :] = pg
        step = 384
        produced = jnp.zeros((S, D), F32)
        back = jnp.zeros((S, D), F32)
        for c in range(0, FF, step):
            h = mm(xs, w1[:, c : c + step])
            sq = h * h
            t = jnp.tanh(0.7978845608028654 * (h + 0.044715 * (h * sq)))
            half = 0.5 * (1.0 + t)
            act = (h * half).astype(BF16)
            slope = half + 0.5 * h * (1.0 - t * t) * (
                0.7978845608028654 * (1.0 + 0.134145 * sq)
            )
            ag = mm(pg, w2[c : c + step, :], 1, 1)
            hg = (ag * slope).astype(BF16)
            act_ref[pl.ds(base, S), c : c + step] = act
            hg_ref[pl.ds(base, S), c : c + step] = hg
            produced = produced + mm(act, w2[c : c + step, :])
            back = back + mm(hg, w1[:, c : c + step], 1, 1)
        rsend[mb, :, 0:CAP, :] = produced.astype(BF16).reshape(G, CAP, D)
        rsend[mb, :, CAP : 2 * CAP, :] = back.astype(BF16).reshape(G, CAP, D)
        exchange(rsend.at[mb], rrecv.at[mb], rsem.at[mb])
        return carry

    lax.fori_loop(0, MB, experts, 0)

    span = FF // L

    def weight_grads(i, carry):
        at = pl.ds(pl.multiple_of(i * span, 128), span)
        g1 = mm(hg_ref[:, at], xr_ref[...], 0, 0).astype(BF16)
        g2 = mm(act_ref[:, at], pr_ref[...], 0, 0).astype(BF16)
        for rr in range(R):
            xg_ref[rr, i, 0] = g1[rr * FS : (rr + 1) * FS]
            xg_ref[rr, i, 1] = g2[rr * FS : (rr + 1) * FS]
        return carry

    lax.fori_loop(0, L, weight_grads, 0)
    for o in range(1, R):
        rr = (r + o) % R
        remote(xg_ref.at[rr], x1_ref.at[R - o - 1], xsem.at[0], part_id(rr)).start()

    acc_ref[...] = jnp.zeros_like(acc_ref)
    small_ref[...] = jnp.zeros_like(small_ref)

    def backward(mb, carry):
        wait_bytes(rrecv.at[mb], rsem.at[mb, 1])
        cols = cols_ref[mb][0:TP]
        prod = rrecv[mb, :, 0:CAP, :].reshape(S, D)
        bgr = rrecv[mb, :, CAP : 2 * CAP, :].reshape(S, D)
        g = g_ref[mb].astype(F32)
        res = res_ref[mb]
        slot_lane = lax.broadcasted_iota(jnp.int32, (TP, S), 1).astype(F32)
        expert_lane = lax.broadcasted_iota(jnp.int32, (TP, G), 1).astype(F32)
        gp = cols[:, 0:G]
        out = res
        gates_grad = jnp.zeros((TP, G), F32)
        picks = []
        for kk in range(2):
            flc = cols[:, G + kk : G + kk + 1]
            keep = cols[:, G + 2 + kk : G + 3 + kk]
            idc = cols[:, G + 4 + kk : G + 5 + kk]
            gate = cols[:, G + 6 + kk : G + 7 + kk]
            pick = jnp.where(slot_lane == flc, 1.0, 0.0)
            picks.append(pick)
            rows = mm(pick.astype(BF16), prod)
            out = out + gate * rows
            gate_grad = jnp.sum(rows * g, axis=-1, keepdims=True) * keep
            gates_grad = gates_grad + jnp.where(expert_lane == idc, gate_grad, 0.0)
        bo_ref[mb] = out
        inner = jnp.sum(gp * gates_grad, axis=-1, keepdims=True)
        logit_grad = (gp * (gates_grad - inner)).astype(BF16)
        ngrad = mm((picks[0] + picks[1]).astype(BF16), bgr) + mm(
            logit_grad, wrt_ref[...]
        )
        small_ref[0:G, :] += mm(logit_grad, n2_ref[mb], 0, 0)
        hat2, rstd2 = normed_of(res)
        small_ref[G + 1 : G + 2, :] += jnp.sum(ngrad * hat2, axis=0, keepdims=True)
        rgrad = g + norm_pull(hat2, rstd2, gain2_ref[...], ngrad)
        branch = rgrad.astype(BF16)
        acc_ref[3 * D : 4 * D, :] += mm(am_ref[mb], branch, 0, 0)
        mgrad = mm(branch, wattn_ref[...], 1, 1).astype(BF16)
        for pair in range(HEADS // 2):
            c = pair * 128
            q = qkv_ref[mb, :, c : c + 128]
            k = qkv_ref[mb, :, D + c : D + c + 128]
            v = qkv_ref[mb, :, 2 * D + c : 2 * D + c + 128]
            mg = mgrad[:, c : c + 128]
            dqs, dks, dvs = [], [], []
            for half in range(2):
                mine = low_half if half == 0 else jnp.logical_not(low_half)
                mgh = jnp.where(mine, mg, jnp.zeros_like(mg))
                p = p_ref[mb, 2 * pair + half]
                dp_ = mm(mgh, v, 1, 1)
                delta = jnp.sum(p * dp_, axis=-1, keepdims=True)
                ds = (p * (dp_ - delta) * HD**-0.5).astype(BF16)
                dqs.append(mm(ds, k))
                dks.append(mm(ds, q, 0, 0))
                dvs.append(mm(p.astype(BF16), mg, 0, 0))
            for n, parts in enumerate((dqs, dks, dvs)):
                dq_ref[:, n * D + c : n * D + c + 128] = jnp.where(
                    low_half, parts[0], parts[1]
                ).astype(BF16)
        n1 = n1_ref[mb]
        for n in range(3):
            acc_ref[n * D : (n + 1) * D, :] += mm(
                n1, dq_ref[:, n * D : (n + 1) * D], 0, 0
            )
        fgrad = mm(dq_ref[...], wqkv_ref[...], 1, 1)
        hat, rstd = normed_of(x_ref[mb].astype(F32))
        small_ref[G : G + 1, :] += jnp.sum(fgrad * hat, axis=0, keepdims=True)
        ig_ref[mb] = rgrad + norm_pull(hat, rstd, gain1_ref[...], fgrad)
        return carry

    lax.fori_loop(0, MB, backward, 0)

    for o in range(1, R):
        wait_bytes(x1_ref.at[o - 1], xsem.at[0, 1])

    def add_slices(i, carry):
        total = xg_ref[r, i].astype(F32)
        for o in range(R - 1):
            total = total + x1_ref[o, i].astype(F32)
        xs_ref[i] = total.astype(BF16)
        return carry

    lax.fori_loop(0, L, add_slices, 0)
    for o in range(1, L):
        i = (j + o) % L
        remote(xs_ref.at[i], eg_ref.at[j], xsem.at[1], plane_id(i)).start()
    pltpu.make_async_copy(xs_ref.at[j], eg_ref.at[j], xsem.at[1, 1]).start()

    for rr in range(R):
        for i in range(L):
            at = (rr * L + i) * NR
            arb_ref[rr, i, 0:NR, :] = acc_ref[at : at + NR, :].astype(BF16)
            if (rr * L + i) * XR < small_ref.shape[0]:
                sat = (rr * L + i) * XR
                arb_ref[rr, i, NR:PR, :] = small_ref[sat : sat + XR, :].astype(BF16)
            else:
                arb_ref[rr, i, NR:PR, :] = jnp.zeros((XR, D), BF16)
    for o in range(1, R):
        rr = (r + o) % R
        remote(arb_ref.at[rr], l1_ref.at[R - o - 1], asem.at[0], part_id(rr)).start()
    for o in range(1, R):
        wait_bytes(l1_ref.at[o - 1], asem.at[0, 1])
    for i in range(L):
        total = arb_ref[r, i].astype(F32)
        for o in range(R - 1):
            total = total + l1_ref[o, i].astype(F32)
        l2s_ref[i] = total.astype(BF16)
    for o in range(1, L):
        i = (j + o) % L
        remote(l2s_ref.at[i], l2_ref.at[L - o - 1], asem.at[1], plane_id(i)).start()
    wait_bytes(l2_ref, asem.at[1, 1])
    total = l2s_ref[j].astype(F32)
    for o in range(L - 1):
        total = total + l2_ref[o].astype(F32)
    l3_ref[z] = total.astype(BF16)
    for o in range(1, Z):
        zz = (z + o) % Z
        remote(l3_ref.at[z], l3_ref.at[z], asem.at[2], (dp, zz)).start()
    wait_bytes(l3_ref.at[pl.ds(0, Z - 1)], asem.at[2, 1])
    total = l3_ref[0].astype(F32)
    for zz in range(1, Z):
        total = total + l3_ref[zz].astype(F32)
    ag_ref[r, j] = total.astype(BF16)
    for o in range(1, L):
        i = (j + o) % L
        remote(ag_ref.at[r, j], ag_ref.at[r, j], asem.at[3], plane_id(i)).start()
    wait_bytes(l2_ref, asem.at[3, 1])
    for o in range(1, R):
        rr = (r + o) % R
        remote(ag_ref.at[r], ag_ref.at[r], asem.at[4], part_id(rr)).start()
    for o in range(1, R):
        wait_bytes(l1_ref.at[o - 1], asem.at[4, 1])
    wait_bytes(eg_ref, xsem.at[1, 1])

    for mb in range(MB):
        wait_bytes(dsend.at[mb, pl.ds(0, G - 1)], dsem.at[mb, 0])
        wait_bytes(rsend.at[mb, pl.ds(0, G - 1)], rsem.at[mb, 0])
    for o in range(1, R):
        wait_bytes(x1_ref.at[o - 1], xsem.at[0, 0])
        wait_bytes(l1_ref.at[o - 1], asem.at[0, 0])
        wait_bytes(l1_ref.at[o - 1], asem.at[4, 0])
    wait_bytes(xs_ref.at[pl.ds(0, L - 1)], xsem.at[1, 0])
    wait_bytes(l2_ref, asem.at[1, 0])
    wait_bytes(l3_ref.at[pl.ds(0, Z - 1)], asem.at[2, 0])
    wait_bytes(l2_ref, asem.at[3, 0])


def on_device(
    groups,
    replicas,
    inputs,
    first_gain,
    w_qkv,
    w_attn,
    second_gain,
    w_router,
    expert_in,
    expert_out,
    expert_ids,
    slot_ids,
    dropped,
    out_grad,
):
    L, _, FF = expert_in.shape
    Z = groups
    R = replicas // L
    G = L * Z
    S = G * CAP
    FS = FF // replicas
    NR = 4 * D // replicas
    PR = NR + XR
    small_rows = -(-(G + 2) // XR) * XR
    rs_rows = -(-(G + 8) // 8) * 8
    pad = ((0, 0), (0, TP - SEQ), (0, 0))
    x = jnp.pad(inputs, pad)
    g = jnp.pad(out_grad, pad)
    swap = lambda a: jnp.transpose(a, (0, 2, 1))
    vmem = pl.BlockSpec(memory_space=pltpu.VMEM)
    hbm = pl.BlockSpec(memory_space=pl.ANY)
    sds = jax.ShapeDtypeStruct
    bo, ig, eg, ag = pl.pallas_call(
        functools.partial(kernel, (L, R, Z, G, FF)),
        out_shape=(
            sds((MB, TP, D), F32),
            sds((MB, TP, D), F32),
            sds((L, 2, FS, D), BF16),
            sds((R, L, PR, D), BF16),
        ),
        in_specs=[vmem] * 10 + [hbm] * 2,
        out_specs=(vmem, vmem, vmem, vmem),
        scratch_shapes=[
            pltpu.VMEM((D, FF), BF16),
            pltpu.VMEM((FF, D), BF16),
            pltpu.VMEM((MB, TP, D), BF16),
            pltpu.VMEM((MB, TP, 3 * D), BF16),
            pltpu.VMEM((MB, HEADS, TP, TP), F32),
            pltpu.VMEM((MB, TP, D), BF16),
            pltpu.VMEM((MB, TP, D), F32),
            pltpu.VMEM((MB, TP, D), BF16),
            pltpu.VMEM((rs_rows, TL), F32),
            pltpu.VMEM((MB, TL, rs_rows), F32),
            pltpu.VMEM((MB, G, 2 * CAP, D), BF16),
            pltpu.VMEM((MB, G, 2 * CAP, D), BF16),
            pltpu.VMEM((MB, G, 2 * CAP, D), BF16),
            pltpu.VMEM((MB, G, 2 * CAP, D), BF16),
            pltpu.VMEM((MB * S, FF), BF16),
            pltpu.VMEM((MB * S, FF), BF16),
            pltpu.VMEM((MB * S, D), BF16),
            pltpu.VMEM((MB * S, D), BF16),
            pltpu.VMEM((R, L, 2, FS, D), BF16),
            pltpu.VMEM((R - 1, L, 2, FS, D), BF16),
            pltpu.VMEM((L, 2, FS, D), BF16),
            pltpu.VMEM((TP, 3 * D), BF16),
            pltpu.VMEM((4 * D, D), F32),
            pltpu.VMEM((small_rows, D), F32),
            pltpu.VMEM((R, L, PR, D), BF16),
            pltpu.VMEM((R - 1, L, PR, D), BF16),
            pltpu.VMEM((L, PR, D), BF16),
            pltpu.VMEM((L - 1, PR, D), BF16),
            pltpu.VMEM((Z, PR, D), BF16),
            pltpu.SemaphoreType.DMA((2,)),
            pltpu.SemaphoreType.DMA((MB, 2)),
            pltpu.SemaphoreType.DMA((MB, 2)),
            pltpu.SemaphoreType.DMA((2, 2)),
            pltpu.SemaphoreType.DMA((5, 2)),
        ],
        compiler_params=pltpu.CompilerParams(
            collective_id=0, has_side_effects=True, vmem_limit_bytes=60 << 20
        ),
        name="block",
    )(
        x,
        g,
        first_gain.reshape(1, D),
        second_gain.reshape(1, D),
        w_qkv,
        w_attn,
        w_router.T,
        swap(expert_ids),
        swap(slot_ids),
        swap(dropped),
        expert_in,
        expert_out,
    )
    parts = ag.reshape(replicas, PR, D)
    dense = parts[:, :NR].reshape(4, D, D).astype(F32)
    small = parts[: small_rows // XR, NR:].reshape(small_rows, D).astype(F32)
    return (
        bo[:, :SEQ],
        ig[:, :SEQ],
        small[G],
        jnp.transpose(dense[:3], (1, 0, 2)).reshape(D, 3 * D),
        dense[3],
        small[G + 1],
        small[:G].T,
        jnp.transpose(eg[:, 0].astype(F32), (0, 2, 1)),
        eg[:, 1].astype(F32),
    )


def solution(mesh):
    rows = P(None, ("dp", "expert"), None)
    split = P("expert", None, None)
    return jax.shard_map(
        functools.partial(on_device, mesh.shape["expert"], mesh.shape["dp"]),
        mesh=mesh,
        in_specs=(
            rows,
            P(),
            P(),
            P(),
            P(),
            P(),
            split,
            split,
            rows,
            rows,
            rows,
            rows,
        ),
        out_specs=(
            rows,
            rows,
            P(),
            P(),
            P(),
            P(),
            P(),
            P("expert", None, "dp"),
            P("expert", "dp", None),
        ),
        check_vma=False,
    )
```

profile of v0, /device:TPU:27, one launch (start us, length us, event | category | flops | bytes accessed | tf_op | source)
XLA Modules:
  0.0 113.3 jit_solution(15080753621889138392)
XLA Ops:
  0.6 0.0 copy-start.3
  0.7 1.3 %reshape.42.gain1_ref = f32[1,384]{1,0:T(1,128)} reshape(f32[384]{0:T(512)} %param.13) | data formatting | bytes 3072 | tf_op jit(solution)/shard_map/reshape | solution.py:518
  1.9 1.2 %reshape.43.gain2_ref = f32[1,384]{1,0:T(1,128)} reshape(f32[384]{0:T(512)} %param.16) | data formatting | bytes 3072 | tf_op jit(solution)/shard_map/reshape | solution.py:519
  3.2 1.0 copy.31
  4.2 0.8 pad.7.x_ref
  4.9 0.0 copy-done.3
  5.0 0.8 pad.8.g_ref
  5.7 97.0 %block.1 = (f32[2,208,384]{2,1,0:T(8,128)}, f32[2,208,384]{2,1,0:T(8,128)}, bf16[4,2,192,384]{3,2,1,0:T(8,128)(2,1)}, bf16[2,4,208,384]{3,2,1,0:T(8,128)(2,1)}) custom-call(bf16[2,208,384]{2,1,0:T(8,128)(2,1)} %pad.7.x_ref, bf16[2,208,384]{2,1,0:T(8,128)(2,1)} %pad.8.g_ref, f32[1,384]{1,0:T(1,128)} %reshape.42.gain1_ref, f32[1,384]{1,0:T(1,128)} %reshape.43.gain2_ref, ...), custom_call_target="tpu_custom_call" | custom-call | tf_op jit(solution)/shard_map/block/pallas_call | solution.py:465
  102.7 0.0 copy-start.1
  102.8 0.0 copy-start.2
  102.8 1.3 %slice.40 = f32[2,197,384]{2,1,0:T(8,128)S(1)} slice(f32[2,208,384]{2,1,0:T(8,128)} %get-tuple-element.13), slice={[0:2], [0:197], [0:384]} | slice | bytes 1210368 | tf_op jit(solution)/shard_map/slice | solution.py:533
  104.0 1.1 copy.34
  105.2 0.0 copy-done.1
  105.2 0.6 slice_reduce_fusion
  105.8 0.6 slice_bitcast_fusion
  106.4 0.0 copy-done.2
  106.4 1.1 copy.35
  107.6 0.2 slice_convert_fusion
  107.7 0.9 slice.57
  108.6 0.1 slice.56
  108.7 1.2 %copy.33 = f32[384,3,384]{0,2,1:T(8,128)S(1)} copy(f32[384,3,384]{2,0,1:T(8,128)S(1)} %bitcast.23) | data formatting | bytes 3538944 | tf_op jit(solution)/shard_map/transpose | solution.py:536
  109.9 0.0 copy-start
  109.9 1.9 %copy.36 = f32[384,1152]{1,0:T(8,128)} copy(f32[384,1152]{0,1:T(8,128)S(1)} %bitcast.24) | data formatting | bytes 3538944
  111.8 0.0 copy-done
  111.8 1.6 %bitcast_convert_fusion = (f32[4,192,384]{2,1,0:T(8,128)}, f32[4,384,192]{1,2,0:T(8,128)}) fusion(bf16[4,2,192,384]{3,2,1,0:T(8,128)(2,1)S(1)} %copy-done), kind=kLoop, calls=%fused_computation.2 | loop fusion | flops 589824 | bytes 3538944 | tf_op jit(solution)/shard_map/convert_element_type | solution.py:541
  (3 shorter events, 0.1 us)
Async XLA Ops:
  0.6 4.3 %copy-start.3 = (bf16[2,197,384]{2,0,1:T(2,128)(2,1)S(1)}, bf16[2,197,384]{2,0,1:T(2,128)(2,1)}, u32[]{:S(2)}) copy-start(bf16[2,197,384]{2,0,1:T(2,128)(2,1)} %param.23) | copy-start | bytes 907780
  102.7 2.4 %copy-start.1 = (bf16[2,4,208,384]{3,2,1,0:T(8,128)(2,1)S(1)}, bf16[2,4,208,384]{3,2,1,0:T(8,128)(2,1)}, u32[]{:S(2)}) copy-start(bf16[2,4,208,384]{3,2,1,0:T(8,128)(2,1)} %get-tuple-element.15) | copy-start | bytes 3833860
  102.8 3.6 %copy-start.2 = (f32[2,208,384]{2,1,0:T(8,128)S(1)}, f32[2,208,384]{2,1,0:T(8,128)}, u32[]{:S(2)}) copy-start(f32[2,208,384]{2,1,0:T(8,128)} %get-tuple-element.14) | copy-start | bytes 1916932
  109.9 1.9 %copy-start = (bf16[4,2,192,384]{3,2,1,0:T(8,128)(2,1)S(1)}, bf16[4,2,192,384]{3,2,1,0:T(8,128)(2,1)}, u32[]{:S(2)}) copy-start(bf16[4,2,192,384]{3,2,1,0:T(8,128)(2,1)} %get-tuple-element.16) | copy-start | bytes 3538948
where the time goes:
time: 114 us; the launch traced here: 113 us
  Pallas kernels  97 us (85%)
  local copies, waits for them, and re-layouts  13.9 us (12%)
  other arithmetic  1.72 us (2%)
    pallas_call x1, Pallas kernels, on_device(): pl.pallas_call(functools.partial(kernel, (L, R, Z, G, FF)), out_shape=(sd...  97 us
    unnamed x13, local copies, waits for them, and re-layouts  5.21 us

commit v1 on v0

v1 whole, which is shorter than its diff:
```python
import functools
import math

import jax
import jax.numpy as jnp
from jax import lax
from jax.experimental import pallas as pl
from jax.experimental.pallas import tpu as pltpu
from jax.sharding import PartitionSpec as P

D = 384
HEADS = 6
HD = 64
SEQ = 197
MB = 2
CAP = 16
EPS = 1e-06
TP = 208
TL = 256
SM = 32
F32 = jnp.float32
BF16 = jnp.bfloat16
MESH = pl.DeviceIdType.MESH
KINDS = ("rows", "gate", "pull", "ggrad", "back", "made")


def mm(a, b, ca=1, cb=0):
    return lax.dot_general(
        a, b, (((ca,), (cb,)), ((), ())), preferred_element_type=F32
    )


def mm_exact(a, b):
    return lax.dot_general(
        a,
        b,
        (((1,), (0,)), ((), ())),
        preferred_element_type=F32,
        precision=lax.Precision.HIGHEST,
    )


def normed_of(rows):
    mean = jnp.sum(rows, axis=-1, keepdims=True) * (1.0 / D)
    centered = rows - mean
    var = jnp.sum(centered * centered, axis=-1, keepdims=True) * (1.0 / D)
    rstd = lax.rsqrt(var + EPS)
    return centered * rstd, rstd


def norm_pull(hat, rstd, gain, grad):
    scaled = grad * gain
    m1 = jnp.sum(scaled, axis=-1, keepdims=True) * (1.0 / D)
    m2 = jnp.sum(scaled * hat, axis=-1, keepdims=True) * (1.0 / D)
    return rstd * (scaled - m1 - hat * m2)


def kernel(dims, ins, outs, scratch):
    L, R, Z, G, FF = dims
    S = G * CAP
    FS = FF // (L * R)
    (
        x_hbm,
        g_hbm,
        gain1_hbm,
        gain2_hbm,
        wqkv_hbm,
        wattn_hbm,
        wrt_hbm,
        ids_hbm,
        slot_hbm,
        drop_hbm,
        win_hbm,
        wout_hbm,
    ) = ins
    bo_ref, ig_ref, eg_ref, *dense_refs, small_out = outs
    x_ref, g_ref, gain1_ref, gain2_ref = scratch["loads"][:4]
    wqkv_ref, wattn_ref, wrt_ref = scratch["loads"][4:7]
    ids_ref, slot_ref, drop_ref, w1, w2 = scratch["loads"][7:]
    n1_ref, qkv_ref, p_ref, am_ref, res_ref, n2_ref = scratch["saved"]
    rs_ref, cols_ref, slope_ref = scratch["work"]
    act_ref, hg_ref, xg_ref, x1_ref, xs_ref, gacc_ref = scratch["expert"]
    dq_ref, acc_ref, small_ref, t1_ref, t2_ref, t3_ref = scratch["grads"]
    lsem, esem, xsem, tsem = scratch["sems"]
    chunks = scratch["chunks"]
    dp = lax.axis_index("dp")
    z = lax.axis_index("expert")
    j = dp // R
    r = dp % R
    me = z * L + j

    def group_id(e):
        return ((e % L) * R + r, e // L)

    def plane_id(i):
        return (i * R + r, z)

    def part_id(rr):
        return (j * R + rr, z)

    def remote(src, dst, send_sem, recv_sem, device):
        pltpu.make_async_remote_copy(
            src_ref=src,
            dst_ref=dst,
            send_sem=send_sem,
            recv_sem=recv_sem,
            device_id=device,
            device_id_type=MESH,
        ).start()

    def wait_bytes(ref, sem):
        pltpu.make_async_copy(ref, ref, sem).wait()

    barrier = pltpu.get_barrier_semaphore()

    @pl.loop(1, G)
    def _(o):
        pl.semaphore_signal(
            barrier, inc=1, device_id=group_id((me + o) % G), device_id_type=MESH
        )

    for o in range(1, R):
        pl.semaphore_signal(
            barrier, inc=1, device_id=part_id((r + o) % R), device_id_type=MESH
        )

    loads = []
    sources = [
        x_hbm,
        g_hbm,
        gain1_hbm,
        gain2_hbm,
        wqkv_hbm,
        wattn_hbm,
        wrt_hbm,
        ids_hbm,
        slot_hbm,
        drop_hbm,
        win_hbm.at[j],
        wout_hbm.at[j],
    ]
    for n, (src, dst) in enumerate(zip(sources, scratch["loads"])):
        loads.append(pltpu.make_async_copy(src, dst, lsem.at[n]))
    for n in (0, 2, 4, 5, 3, 6, 7, 8, 9, 1, 10, 11):
        loads[n].start()

    def ready(*which):
        for n in which:
            loads[n].wait()

    low_half = lax.broadcasted_iota(jnp.int32, (TP, 128), 1) < HD
    key_ok = lax.broadcasted_iota(jnp.int32, (TP, TP), 1) < SEQ
    slot_lane = lax.broadcasted_iota(
        jnp.int32, (G, CAP, 128), 2
    ) == lax.broadcasted_iota(jnp.int32, (G, CAP, 128), 1)

    def exchange(kind, mb):
        send, recv = scratch[kind]
        send, recv = send.at[mb], recv.at[mb]
        n = KINDS.index(kind)
        pltpu.make_async_copy(send.at[me], recv.at[me], esem.at[n, mb, 1]).start()

        @pl.loop(1, G)
        def _(o):
            e = (me + o) % G
            remote(
                send.at[e],
                recv.at[me],
                esem.at[n, mb, 0],
                esem.at[n, mb, 1],
                group_id(e),
            )

    def arrived(kind, mb):
        recv = scratch[kind][1].at[mb]
        wait_bytes(recv, esem.at[KINDS.index(kind), mb, 1])
        return recv

    def row_of_slots(col):
        spread = jnp.where(slot_lane, col.reshape(G, CAP, 1), 0.0)
        return jnp.sum(spread, axis=1, keepdims=True)

    def slots_of_row(row):
        spread = jnp.where(slot_lane, row, 0.0)
        return jnp.sum(spread, axis=-1, keepdims=True).reshape(S, 1)

    def forward(mb):
        if mb == 0:
            ready(0, 2, 4)
        x = x_ref[mb].astype(F32)
        hat, _ = normed_of(x)
        n1 = (hat * gain1_ref[...].reshape(1, D)).astype(BF16)
        n1_ref[mb] = n1
        qkv_ref[mb] = mm(n1, wqkv_ref[...]).astype(BF16)
        for pair in range(HEADS // 2):
            c = pair * 128
            q = qkv_ref[mb, :, c : c + 128] * jnp.asarray(HD**-0.5, BF16)
            k = qkv_ref[mb, :, D + c : D + c + 128]
            v = qkv_ref[mb, :, 2 * D + c : 2 * D + c + 128]
            mixed = []
            for half in range(2):
                mine = low_half if half == 0 else jnp.logical_not(low_half)
                qh = jnp.where(mine, q, jnp.zeros_like(q))
                s = mm(qh, k, 1, 1)
                s = jnp.where(key_ok, s, -1e30)
                e = jnp.exp(s - jnp.max(s, axis=-1, keepdims=True))
                p = e / jnp.sum(e, axis=-1, keepdims=True)
                p_ref[mb, 2 * pair + half] = p
                mixed.append(mm(p.astype(BF16), v))
            am_ref[mb, :, c : c + 128] = jnp.where(
                low_half, mixed[0], mixed[1]
            ).astype(BF16)
        if mb == 0:
            ready(5, 3, 6, 7, 8, 9, 1)
        res = x + mm(am_ref[mb], wattn_ref[...])
        res_ref[mb] = res
        hat2, _ = normed_of(res)
        n2 = (hat2 * gain2_ref[...].reshape(1, D)).astype(BF16)
        n2_ref[mb] = n2
        logits = mm(wrt_ref[...], n2, 1, 1)
        ex = jnp.exp(logits - jnp.max(logits, axis=0, keepdims=True))
        gp = ex / jnp.sum(ex, axis=0, keepdims=True)
        ids = ids_ref[mb]
        drop = drop_ref[mb]
        slot = slot_ref[mb]
        flat = jnp.where(drop == 0, ids * CAP + slot, S)
        rs_ref[...] = jnp.zeros_like(rs_ref)
        rs_ref[0:G, 0:TP] = gp
        rs_ref[G : G + 2, 0:TP] = jnp.full((2, TP), S, F32)
        rs_ref[G : G + 2, 0:SEQ] = flat.astype(F32)
        rs_ref[G + 2 : G + 4, 0:SEQ] = 1.0 - drop.astype(F32)
        rs_ref[G + 4 : G + 6, 0:SEQ] = ids.astype(F32)
        rs_ref[G + 8 : G + 10, 0:SEQ] = slot.astype(F32)
        expert_of = lax.broadcasted_iota(jnp.int32, (G, TP), 0).astype(F32)
        slot_of = lax.broadcasted_iota(jnp.int32, (S, TP), 0).astype(F32)
        pick = jnp.zeros((S, TP), F32)
        gcol = jnp.zeros((S, 1), F32)
        for kk in range(2):
            flr = rs_ref[G + kk : G + kk + 1, 0:TP]
            keep = rs_ref[G + 2 + kk : G + 3 + kk, 0:TP]
            idr = rs_ref[G + 4 + kk : G + 5 + kk, 0:TP]
            mine = jnp.where(expert_of == idr, gp, 0.0)
            gate = jnp.sum(mine, axis=0, keepdims=True) * keep
            rs_ref[G + 6 + kk : G + 7 + kk, 0:TP] = gate
            hit = slot_of == flr
            pick = pick + jnp.where(hit, 1.0, 0.0)
            gcol = gcol + jnp.sum(jnp.where(hit, gate, 0.0), axis=-1, keepdims=True)
        cols_ref[mb] = rs_ref[...].T
        pick = pick.astype(BF16)
        scratch["rows"][0][mb] = mm(pick, n2).astype(BF16).reshape(G, CAP, D)
        scratch["gate"][0][mb] = row_of_slots(gcol)
        scratch["pull"][0][mb] = mm(pick, g_ref[mb]).astype(BF16).reshape(G, CAP, D)

    def experts(mb):
        xs = arrived("rows", mb)[...].reshape(S, D)
        step = 384
        produced = jnp.zeros((S, D), F32)
        for c in range(0, FF, step):
            h = mm(xs, w1[:, c : c + step])
            sq = h * h
            t = jnp.tanh(0.7978845608028654 * (h + 0.044715 * (h * sq)))
            half = 0.5 * (1.0 + t)
            act = (h * half).astype(BF16)
            slope_ref[:, c : c + step] = half + 0.5 * h * (1.0 - t * t) * (
                0.7978845608028654 * (1.0 + 0.134145 * sq)
            )
            act_ref[mb, :, c : c + step] = act
            produced = produced + mm(act, w2[c : c + step, :])
        produced = produced.astype(BF16)
        scratch["made"][0][mb] = produced.reshape(G, CAP, D)
        gates = slots_of_row(arrived("gate", mb)[...])
        grow = arrived("pull", mb)[...].reshape(S, D).astype(F32)
        pg = (gates * grow).astype(BF16)
        scratch["gated"][mb] = pg
        gg = jnp.sum(grow * produced.astype(F32), axis=-1, keepdims=True)
        scratch["ggrad"][0][mb] = row_of_slots(gg)
        back = jnp.zeros((S, D), F32)
        for c in range(0, FF, step):
            ag = mm(pg, w2[c : c + step, :], 1, 1)
            hg = (ag * slope_ref[:, c : c + step]).astype(BF16)
            hg_ref[mb, :, c : c + step] = hg
            back = back + mm(hg, w1[:, c : c + step], 1, 1)
        scratch["back"][0][mb] = back.astype(BF16).reshape(G, CAP, D)
        exchange("ggrad", mb)
        exchange("back", mb)

    span = FF // L

    def weight_grads(mb):
        xs = scratch["rows"][1][mb].reshape(S, D)
        pg = scratch["gated"][mb]

        def part(i, carry):
            at = pl.ds(pl.multiple_of(i * span, 128), span)
            g1 = mm(hg_ref[mb, :, at], xs, 0, 0)
            g2 = mm(act_ref[mb, :, at], pg, 0, 0)
            if mb < MB - 1:
                if mb > 0:
                    g1 = g1 + gacc_ref[0, i]
                    g2 = g2 + gacc_ref[1, i]
                gacc_ref[0, i] = g1
                gacc_ref[1, i] = g2
            else:
                g1 = (g1 + gacc_ref[0, i]).astype(BF16)
                g2 = (g2 + gacc_ref[1, i]).astype(BF16)
                for rr in range(R):
                    xg_ref[rr, i, 0] = g1[rr * FS : (rr + 1) * FS]
                    xg_ref[rr, i, 1] = g2[rr * FS : (rr + 1) * FS]
            return carry

        lax.fori_loop(0, L, part, 0)

    def swap_slices():
        for o in range(1, R):
            rr = (r + o) % R
            remote(
                xg_ref.at[rr],
                x1_ref.at[R - o - 1],
                xsem.at[0, 0],
                xsem.at[0, 1],
                part_id(rr),
            )

    def add_slices():
        if R > 1:
            wait_bytes(x1_ref, xsem.at[0, 1])

        def part(i, carry):
            total = xg_ref[r, i].astype(F32)
            for o in range(R - 1):
                total = total + x1_ref[o, i].astype(F32)
            xs_ref[i] = total.astype(BF16)
            return carry

        lax.fori_loop(0, L, part, 0)

    def hand_out(mat):
        for o in range(1, L):
            i = (j + o) % L
            remote(
                xs_ref.at[i, mat],
                eg_ref.at[j, mat],
                xsem.at[1 + mat, 0],
                xsem.at[1 + mat, 1],
                plane_id(i),
            )
        pltpu.make_async_copy(
            xs_ref.at[j, mat], eg_ref.at[j, mat], xsem.at[1 + mat, 1]
        ).start()

    def add_block(block, value):
        for ck in chunks:
            if block in ck["blocks"]:
                src, pr = ck["src"], ck["pr"]
                at = ck["blocks"].index(block) * (D // pr)
        if pr % 8 == 0:
            value = value.reshape(D // pr, pr, D)
            src[at : at + D // pr] = value.astype(BF16)
        else:
            acc_ref[block * D : (block + 1) * D] = value
            rows = math.lcm(pr, 8)

            @pl.loop(0, D // rows)
            def _(n):
                first = pl.multiple_of(block * D + n * rows, 8)
                piece = acc_ref[pl.ds(first, rows)].astype(BF16)
                for m in range(rows // pr):
                    src[at + n * (rows // pr) + m] = piece[m * pr : (m + 1) * pr]

    def sum_start(ck):
        for n in range(1, L + 1):
            i = (j + n) % L
            for o in range(1, R):
                rr = (r + o) % R
                remote(
                    ck["src"].at[pl.ds((rr * L + i) * Z, Z)],
                    ck["l1"].at[R - o - 1, i],
                    ck["send"].at[0],
                    ck["s1"].at[R - o - 1, i],
                    part_id(rr),
                )

    def sum_pairs(ck):
        for n in range(1, L + 1):
            i = (j + n) % L
            total = ck["src"][pl.ds((r * L + i) * Z, Z)].astype(F32)
            for o in range(R - 1):
                wait_bytes(ck["l1"].at[o, i], ck["s1"].at[o, i])
                total = total + ck["l1"][o, i].astype(F32)
            ck["l2s"][i] = total.astype(BF16)
            if n < L:
                remote(
                    ck["l2s"].at[i],
                    ck["l2"].at[L - n - 1],
                    ck["send"].at[1],
                    ck["recv"].at[1],
                    plane_id(i),
                )

    def sum_plane(ck):
        if L > 1:
            wait_bytes(ck["l2"], ck["recv"].at[1])
        for n in range(Z - 1, -1, -1):
            zz = (z + n) % Z
            total = ck["l2s"][j, zz].astype(F32)
            for o in range(L - 1):
                total = total + ck["l2"][o, zz].astype(F32)
            ck["l3s"][zz] = total.astype(BF16)
            if n > 0:
                remote(
                    ck["l3s"].at[zz],
                    ck["l3"].at[Z - n - 1],
                    ck["send"].at[2],
                    ck["recv"].at[2],
                    (dp, zz),
                )

    def sum_z(ck):
        out = ck["out"]
        if Z > 1:
            wait_bytes(ck["l3"], ck["recv"].at[2])
        total = ck["l3s"][z].astype(F32)
        for o in range(Z - 1):
            total = total + ck["l3"][o].astype(F32)
        mine = (r * L + j) * Z + z
        out[mine] = total.astype(BF16)
        for n in range(Z - 1, 0, -1):
            remote(
                out.at[mine],
                out.at[mine],
                ck["send"].at[3],
                ck["recv"].at[3],
                (dp, (z + n) % Z),
            )

    def spread_plane(ck):
        out = ck["out"]
        if Z > 1:
            wait_bytes(ck["l3"], ck["recv"].at[3])
        mine = pl.ds((r * L + j) * Z, Z)
        for n in range(1, L):
            remote(
                out.at[mine],
                out.at[mine],
                ck["send"].at[4],
                ck["s2"].at[L - n - 1],
                plane_id((j + n) % L),
            )
        spread_part(ck, j)

    def spread_part(ck, i):
        out = ck["out"]
        at = pl.ds((r * L + i) * Z, Z)
        for o in range(1, R):
            remote(
                out.at[at],
                out.at[at],
                ck["send"].at[5],
                ck["recv"].at[5],
                part_id((r + o) % R),
            )

    def spread_parts(ck):
        for n in range(1, L):
            wait_bytes(ck["l2"].at[n - 1], ck["s2"].at[n - 1])
            spread_part(ck, (j + n) % L)

    def sum_end(ck):
        if R > 1:
            wait_bytes(ck["l1"], ck["recv"].at[5])
            wait_bytes(ck["l1"], ck["send"].at[0])
            wait_bytes(ck["l1"], ck["send"].at[5])
        if L > 1:
            wait_bytes(ck["l2"], ck["send"].at[1])
            wait_bytes(ck["l2"], ck["send"].at[4])
        if Z > 1:
            wait_bytes(ck["l3"], ck["send"].at[2])
            wait_bytes(ck["l3"], ck["send"].at[3])

    levels = ((t1_ref, r, R, part_id), (t2_ref, j, L, plane_id), (t3_ref, z, Z, None))

    def small_start(level):
        buf, at, count, ident = levels[level]
        for o in range(1, count):
            to = (at + o) % count
            remote(
                buf.at[at],
                buf.at[at],
                tsem.at[level, 0],
                tsem.at[level, 1],
                (dp, to) if ident is None else ident(to),
            )

    def small_sum(level):
        buf, _, count, _ = levels[level]
        if count > 1:
            wait_bytes(buf.at[pl.ds(0, count - 1)], tsem.at[level, 1])
        total = buf[0].astype(F32)
        for n in range(1, count):
            total = total + buf[n].astype(F32)
        return total

    def small_next(level):
        total = small_sum(level)
        buf, at, _, _ = levels[level + 1]
        buf[at] = total.astype(BF16)
        small_start(level + 1)

    def small_end():
        small_out[...] = small_sum(2)
        for level in range(3):
            buf, _, count, _ = levels[level]
            if count > 1:
                wait_bytes(buf.at[pl.ds(0, count - 1)], tsem.at[level, 0])

    last = MB - 1

    def add_grad(mb, block, value):
        at = slice(block * D, (block + 1) * D)
        if mb > 0:
            value = value + acc_ref[at]
        if mb < last:
            acc_ref[at] = value
        else:
            add_block(block, value)

    def add_small(mb, at, value):
        small_ref[at] = value if mb == 0 else small_ref[at] + value

    def cols_of(mb):
        cols = cols_ref[mb][0:TP]
        col = lambda n: cols[:, n : n + 1]
        return cols, col

    def backward(mb):
        cols, col = cols_of(mb)
        ggr = arrived("ggrad", mb)[...].reshape(G, 128)
        g = g_ref[mb].astype(F32)
        res = res_ref[mb]
        slot_at = lax.broadcasted_iota(jnp.int32, (TP, S), 1).astype(F32)
        lane_at = lax.broadcasted_iota(jnp.int32, (TP, 128), 1).astype(F32)
        expert_at = lax.broadcasted_iota(jnp.int32, (TP, G), 1).astype(F32)
        gp = cols[:, 0:G]
        gates_grad = jnp.zeros((TP, G), F32)
        pick = jnp.zeros((TP, S), F32)
        for kk in range(2):
            keep = col(G + 2 + kk)
            named = jnp.where(expert_at == col(G + 4 + kk), 1.0, 0.0)
            of_slot = jnp.where(
                lane_at == col(G + 8 + kk), mm_exact(named, ggr), 0.0
            )
            gate_grad = jnp.sum(of_slot, axis=-1, keepdims=True) * keep
            gates_grad = gates_grad + named * gate_grad
            pick = pick + jnp.where(slot_at == col(G + kk), 1.0, 0.0)
        inner = jnp.sum(gp * gates_grad, axis=-1, keepdims=True)
        logit_grad = (gp * (gates_grad - inner)).astype(BF16)
        add_small(mb, slice(0, G), mm(logit_grad, n2_ref[mb], 0, 0))
        bgr = arrived("back", mb)[...].reshape(S, D)
        ngrad = mm(pick.astype(BF16), bgr) + mm(logit_grad, wrt_ref[...])
        hat2, rstd2 = normed_of(res)
        add_small(
            mb, slice(G, G + 1), jnp.sum(ngrad * hat2, axis=0, keepdims=True)
        )
        gain2 = gain2_ref[...].reshape(1, D)
        rgrad = g + norm_pull(hat2, rstd2, gain2, ngrad)
        branch = rgrad.astype(BF16)
        add_grad(mb, 3, mm(am_ref[mb], branch, 0, 0))
        mgrad = mm(branch, wattn_ref[...], 1, 1).astype(BF16)
        for pair in range(HEADS // 2):
            c = pair * 128
            mg = mgrad[:, c : c + 128]
            dvs = [
                mm(p_ref[mb, 2 * pair + half].astype(BF16), mg, 0, 0)
                for half in range(2)
            ]
            dq_ref[:, 2 * D + c : 2 * D + c + 128] = jnp.where(
                low_half, dvs[0], dvs[1]
            ).astype(BF16)
        n1 = n1_ref[mb]
        add_grad(mb, 2, mm(n1, dq_ref[:, 2 * D : 3 * D], 0, 0))
        if mb == last and len(chunks) > 1:
            sum_start(chunks[0])
        for pair in range(HEADS // 2):
            c = pair * 128
            q = qkv_ref[mb, :, c : c + 128]
            k = qkv_ref[mb, :, D + c : D + c + 128]
            v = qkv_ref[mb, :, 2 * D + c : 2 * D + c + 128]
            mg = mgrad[:, c : c + 128]
            dqs, dks = [], []
            for half in range(2):
                mine = low_half if half == 0 else jnp.logical_not(low_half)
                mgh = jnp.where(mine, mg, jnp.zeros_like(mg))
                p = p_ref[mb, 2 * pair + half]
                dp_ = mm(mgh, v, 1, 1)
                delta = jnp.sum(p * dp_, axis=-1, keepdims=True)
                ds = (p * (dp_ - delta) * HD**-0.5).astype(BF16)
                dqs.append(mm(ds, k))
                dks.append(mm(ds, q, 0, 0))
            for n, parts in enumerate((dqs, dks)):
                dq_ref[:, n * D + c : n * D + c + 128] = jnp.where(
                    low_half, parts[0], parts[1]
                ).astype(BF16)
        for n in range(2):
            add_grad(mb, n, mm(n1, dq_ref[:, n * D : (n + 1) * D], 0, 0))
        if mb == last:
            sum_start(chunks[-1])
            if len(chunks) > 1:
                sum_pairs(chunks[0])
        fgrad = mm(dq_ref[...], wqkv_ref[...], 1, 1)
        hat, rstd = normed_of(x_ref[mb].astype(F32))
        add_small(
            mb, slice(G + 1, G + 2), jnp.sum(fgrad * hat, axis=0, keepdims=True)
        )
        gain1 = gain1_ref[...].reshape(1, D)
        ig_ref[mb] = rgrad + norm_pull(hat, rstd, gain1, fgrad)

    def combine(mb):
        _, col = cols_of(mb)
        made = arrived("made", mb)[...].reshape(S, D)
        slot_at = lax.broadcasted_iota(jnp.int32, (TP, S), 1).astype(F32)
        out = res_ref[mb]
        for kk in range(2):
            pick = jnp.where(slot_at == col(G + kk), 1.0, 0.0).astype(BF16)
            out = out + col(G + 6 + kk) * mm(pick, made)
        bo_ref[mb] = out

    forward(0)
    pl.semaphore_wait(barrier, G - 1 + R - 1)
    for kind in ("rows", "gate", "pull"):
        exchange(kind, 0)
    for mb in range(1, MB):
        forward(mb)
        for kind in ("rows", "gate", "pull"):
            exchange(kind, mb)
    ready(10, 11)
    for mb in range(MB):
        experts(mb)
        if mb == last:
            for m in range(MB):
                exchange("made", m)
        weight_grads(mb)
    swap_slices()
    small_ref[...] = jnp.zeros_like(small_ref)
    for mb in range(MB):
        backward(mb)
        if mb == 0:
            add_slices()
            hand_out(0)
    t1_ref[r] = small_ref[...].astype(BF16)
    small_start(0)
    if len(chunks) > 1:
        sum_plane(chunks[0])
    sum_pairs(chunks[-1])
    small_next(0)
    if len(chunks) > 1:
        sum_z(chunks[0])
    combine(0)
    sum_plane(chunks[-1])
    small_next(1)
    hand_out(1)
    if len(chunks) > 1:
        spread_plane(chunks[0])
    for mb in range(1, MB):
        combine(mb)
    sum_z(chunks[-1])
    if len(chunks) > 1:
        spread_parts(chunks[0])
    spread_plane(chunks[-1])
    spread_parts(chunks[-1])
    small_end()
    for ck in chunks:
        sum_end(ck)

    for mat in range(2):
        wait_bytes(xs_ref.at[pl.ds(0, L), 0], xsem.at[1 + mat, 1])
        if L > 1:
            wait_bytes(xs_ref.at[pl.ds(0, L - 1), 0], xsem.at[1 + mat, 0])
    if R > 1:
        wait_bytes(x1_ref, xsem.at[0, 0])
    for n, kind in enumerate(KINDS):
        for mb in range(MB):
            sent = scratch[kind][0].at[mb, pl.ds(0, G - 1)]
            wait_bytes(sent, esem.at[n, mb, 0])


def on_device(
    groups,
    replicas,
    inputs,
    first_gain,
    w_qkv,
    w_attn,
    second_gain,
    w_router,
    expert_in,
    expert_out,
    expert_ids,
    slot_ids,
    dropped,
    out_grad,
):
    L, _, FF = expert_in.shape
    Z = groups
    R = replicas // L
    G = L * Z
    S = G * CAP
    FS = FF // replicas
    parts = R * L * Z
    groups_of_blocks = [(2, 3), (0, 1)]
    if 2 * D % parts or (2 * D // parts) % 8:
        groups_of_blocks = [(0, 1, 2, 3)]
    small_rows = -(-(G + 2) // SM) * SM
    rs_rows = -(-(G + 10) // 8) * 8
    pad = ((0, 0), (0, TP - SEQ), (0, 0))
    swap = lambda a: jnp.transpose(a, (0, 2, 1))
    operands = (
        jnp.pad(inputs, pad),
        jnp.pad(out_grad, pad),
        first_gain,
        second_gain,
        w_qkv,
        w_attn,
        w_router.T,
        swap(expert_ids),
        swap(slot_ids),
        swap(dropped),
        expert_in,
        expert_out,
    )
    vmem = pl.BlockSpec(memory_space=pltpu.VMEM)
    hbm = pl.BlockSpec(memory_space=pl.ANY)
    sds = jax.ShapeDtypeStruct
    V = pltpu.VMEM
    dma = pltpu.SemaphoreType.DMA
    scratch = {
        "loads": [V(a.shape, a.dtype) for a in operands[:10]]
        + [V((D, FF), BF16), V((FF, D), BF16)],
        "saved": [
            V((MB, TP, D), BF16),
            V((MB, TP, 3 * D), BF16),
            V((MB, HEADS, TP, TP), F32),
            V((MB, TP, D), BF16),
            V((MB, TP, D), F32),
            V((MB, TP, D), BF16),
        ],
        "work": [
            V((rs_rows, TL), F32),
            V((MB, TL, rs_rows), F32),
            V((S, FF), F32),
        ],
        "expert": [
            V((MB, S, FF), BF16),
            V((MB, S, FF), BF16),
            V((R, L, 2, FS, D), BF16),
            V((max(R - 1, 1), L, 2, FS, D), BF16),
            V((L, 2, FS, D), BF16),
            V((2, L, FF // L, D), F32),
        ],
        "grads": [
            V((TP, 3 * D), BF16),
            V((4 * D, D), F32),
            V((small_rows, D), F32),
            V((R, small_rows, D), BF16),
            V((L, small_rows, D), BF16),
            V((Z, small_rows, D), BF16),
        ],
        "gated": V((MB, S, D), BF16),
        "sems": [dma((12,)), dma((len(KINDS), MB, 2)), dma((3, 2)), dma((3, 2))],
    }
    for kind in KINDS:
        slim = kind in ("gate", "ggrad")
        shape = (MB, G, 1, 128) if slim else (MB, G, CAP, D)
        scratch[kind] = [V(shape, F32 if slim else BF16)] * 2
    scratch["chunks"] = []
    for blocks in groups_of_blocks:
        pr = len(blocks) * D // parts
        scratch["chunks"].append(
            {
                "src": V((parts, pr, D), BF16),
                "l1": V((max(R - 1, 1), L, Z, pr, D), BF16),
                "l2s": V((L, Z, pr, D), BF16),
                "l2": V((max(L - 1, 1), Z, pr, D), BF16),
                "l3s": V((Z, pr, D), BF16),
                "l3": V((max(Z - 1, 1), pr, D), BF16),
                "s1": dma((max(R - 1, 1), L)),
                "s2": dma((max(L - 1, 1),)),
                "send": dma((6,)),
                "recv": dma((6,)),
            }
        )
    leaves, tree = jax.tree.flatten(scratch)
    n_in, n_out = len(operands), 4 + len(groups_of_blocks)

    def body(*refs):
        ins, outs = refs[:n_in], refs[n_in : n_in + n_out]
        held = jax.tree.unflatten(tree, refs[n_in + n_out :])
        for n, blocks in enumerate(groups_of_blocks):
            ck = held["chunks"][n]
            ck["blocks"] = list(blocks)
            ck["out"] = outs[3 + n]
            ck["pr"] = len(blocks) * D // parts
        kernel((L, R, Z, G, FF), ins, outs, held)

    bo, ig, eg, *dense, small = pl.pallas_call(
        body,
        out_shape=(
            sds((MB, TP, D), F32),
            sds((MB, TP, D), F32),
            sds((L, 2, FS, D), BF16),
            *(
                sds((parts, len(blocks) * D // parts, D), BF16)
                for blocks in groups_of_blocks
            ),
            sds((small_rows, D), F32),
        ),
        in_specs=[hbm] * n_in,
        out_specs=[vmem] * n_out,
        scratch_shapes=leaves,
        compiler_params=pltpu.CompilerParams(
            collective_id=0, has_side_effects=True, vmem_limit_bytes=63 << 20
        ),
        name="block",
    )(*operands)
    blocks = {}
    for names, got in zip(groups_of_blocks, dense):
        got = got.reshape(len(names), D, D).astype(F32)
        for n, name in enumerate(names):
            blocks[name] = got[n]
    return (
        bo[:, :SEQ],
        ig[:, :SEQ],
        small[G + 1],
        jnp.concatenate([blocks[n] for n in range(3)], axis=1),
        blocks[3],
        small[G],
        small[:G].T,
        jnp.transpose(eg[:, 0].astype(F32), (0, 2, 1)),
        eg[:, 1].astype(F32),
    )


def solution(mesh):
    rows = P(None, ("dp", "expert"), None)
    split = P("expert", None, None)
    return jax.shard_map(
        functools.partial(on_device, mesh.shape["expert"], mesh.shape["dp"]),
        mesh=mesh,
        in_specs=(
            rows,
            P(),
            P(),
            P(),
            P(),
            P(),
            split,
            split,
            rows,
            rows,
            rows,
            rows,
        ),
        out_specs=(
            rows,
            rows,
            P(),
            P(),
            P(),
            P(),
            P(),
            P("expert", None, "dp"),
            P("expert", "dp", None),
        ),
        check_vma=False,
    )
```

time: 114 us -> 86.4 us (0.76)
  the two profiles are of different devices: /device:TPU:27 before, /device:TPU:0 now
where the time goes in v1:
time: 86.4 us; the launch traced here: 86.2 us
  Pallas kernels  72.9 us (84%)
  local copies, waits for them, and re-layouts  9.69 us (11%)
  other arithmetic  2.88 us (3%)
    pallas_call x1, Pallas kernels, on_device(): pl.pallas_call(body, out_shape=(sds((MB, TP, D), F32), sds((MB, TP, D), F...  72.9 us
    unnamed x14, local copies, waits for them, and re-layouts  4.78 us

profile of v1, /device:TPU:0, one launch (start us, length us, event | category | flops | bytes accessed | tf_op | source)
XLA Modules:
  0.0 86.2 jit_solution(7712674489967788585)
XLA Ops:
  0.6 1.0 %copy.21 = bf16[2,197,384]{2,1,0:T(8,128)(2,1)S(1)} copy(bf16[2,197,384]{2,0,1:T(2,128)(2,1)} %param.12) | data formatting | bytes 605184 | tf_op args[0]
  1.6 0.8 pad.7.refs_0_
  2.4 1.0 %copy.22 = bf16[2,197,384]{2,1,0:T(8,128)(2,1)S(1)} copy(bf16[2,197,384]{2,0,1:T(2,128)(2,1)} %param.23) | data formatting | bytes 605184 | tf_op args[11]
  3.4 0.8 pad.8.refs_1_
  4.2 72.9 %block.1 = (f32[2,208,384]{2,1,0:T(8,128)}, f32[2,208,384]{2,1,0:T(8,128)}, bf16[4,2,192,384]{3,2,1,0:T(8,128)(2,1)}, bf16[32,24,384]{2,1,0:T(8,128)(2,1)}, bf16...) custom-call(bf16[2,208,384]{2,1,0:T(8,128)(2,1)} %pad.7.refs_0_, bf16[2,208,384]{2,1,0:T(8,128)(2,1)} %pad.8.refs_1_, ...), custom_call_target="tpu_custom_call" | custom-call | tf_op jit(solution)/shard_map/block/pallas_call | solution.py:804
  77.1 0.0 copy-start.4
  77.1 0.0 copy-start.3
  77.1 1.2 %slice.37 = f32[2,197,384]{2,1,0:T(8,128)S(1)} slice(f32[2,208,384]{2,1,0:T(8,128)} %get-tuple-element.15), slice={[0:2], [0:197], [0:384]} | slice | bytes 1210368 | tf_op jit(solution)/shard_map/slice | solution.py:830
  78.3 0.0 copy-start
  78.3 0.0 copy-start.1
  78.3 1.1 %copy.23 = f32[2,197,384]{2,0,1:T(2,128)} copy(f32[2,197,384]{2,1,0:T(8,128)S(1)} %slice.37) | data formatting | bytes 1210368
  79.4 0.0 copy-done.4
  79.4 0.6 slice_reduce_fusion
  80.0 0.6 slice_bitcast_fusion
  80.6 0.0 copy-done.3
  80.7 1.1 %copy.24 = f32[2,197,384]{2,0,1:T(2,128)} copy(f32[2,197,384]{2,1,0:T(8,128)S(1)} %slice.38) | data formatting | bytes 1210368
  81.8 0.0 copy-done
  81.8 0.0 copy-done.1
  81.8 1.0 %fusion = (f32[16,24,384]{2,1,0:T(8,128)}, f32[16,24,384]{2,1,0:T(8,128)S(1)}, f32[16,24,384]{2,1,0:T(8,128)S(1)}, f32[16,24,384]{2,1,0:T(8,128)S(1)}) fusion(bf16[32,24,384]{2,1,0:T(8,128)(2,1)S(1)} %copy-done, bf16[32,24,384]{2,1,0:T(8,128)(2,1)S(1)} %copy-done.1), kind=kLoop, calls=%fused_computation.6 | loop fusion | bytes 4718592 | tf_op jit(solution)/shard_map/slice | solution.py:828
  82.8 0.0 copy-start.2
  82.8 1.3 %pad_maximum_fusion = f32[384,1152]{1,0:T(8,128)} fusion(f32[384,384]{1,0:T(8,128)S(1)} %bitcast.18, f32[384,384]{1,0:T(8,128)S(1)} %bitcast.19, f32[384,384]{1,0:T(8,128)S(1)} %bitcast.20), kind=kLoop, calls=%fused_computation | loop fusion | flops 884736 | bytes 3538944 | tf_op jit(solution)/shard_map/concatenate | solution.py:833
  84.1 0.5 copy-done.2
  84.6 1.6 %bitcast_convert_fusion = (f32[4,192,384]{2,1,0:T(8,128)}, f32[4,384,192]{1,2,0:T(8,128)}) fusion(bf16[4,2,192,384]{3,2,1,0:T(8,128)(2,1)S(1)} %copy-done.2), kind=kLoop, calls=%fused_computation.2 | loop fusion | flops 589824 | bytes 3538944 | tf_op jit(solution)/shard_map/convert_element_type | solution.py:838
  (1 shorter events, 0.0 us)
Async XLA Ops:
  77.1 2.4 %copy-start.4 = (f32[32,384]{1,0:T(8,128)S(1)}, f32[32,384]{1,0:T(8,128)}, u32[]{:S(2)}) copy-start(f32[32,384]{1,0:T(8,128)} %get-tuple-element.17) | copy-start | bytes 147460
  77.1 3.6 %copy-start.3 = (f32[2,208,384]{2,1,0:T(8,128)S(1)}, f32[2,208,384]{2,1,0:T(8,128)}, u32[]{:S(2)}) copy-start(f32[2,208,384]{2,1,0:T(8,128)} %get-tuple-element.16) | copy-start | bytes 1916932
  78.3 3.5 %copy-start = (bf16[32,24,384]{2,1,0:T(8,128)(2,1)S(1)}, bf16[32,24,384]{2,1,0:T(8,128)(2,1)}, u32[]{:S(2)}) copy-start(bf16[32,24,384]{2,1,0:T(8,128)(2,1)} %get-tuple-element.19) | copy-start | bytes 1769476
  78.3 3.5 %copy-start.1 = (bf16[32,24,384]{2,1,0:T(8,128)(2,1)S(1)}, bf16[32,24,384]{2,1,0:T(8,128)(2,1)}, u32[]{:S(2)}) copy-start(bf16[32,24,384]{2,1,0:T(8,128)(2,1)} %get-tuple-element.18) | copy-start | bytes 1769476
  82.8 1.8 %copy-start.2 = (bf16[4,2,192,384]{3,2,1,0:T(8,128)(2,1)S(1)}, bf16[4,2,192,384]{3,2,1,0:T(8,128)(2,1)}, u32[]{:S(2)}) copy-start(bf16[4,2,192,384]{3,2,1,0:T(8,128)(2,1)} %get-tuple-element.20) | copy-start | bytes 3538948

commit v2 on v1

--- a/solution.py
+++ b/solution.py
@@ -18,6 +18,8 @@
 TP = 208
 TL = 256
 SM = 32
+ROWS = (D, D, 256, 256, 256)
+START = (0, D, 2 * D, 2 * D + 256, 2 * D + 512)
 F32 = jnp.float32
 BF16 = jnp.bfloat16
 MESH = pl.DeviceIdType.MESH
@@ -73,13 +75,14 @@
         win_hbm,
         wout_hbm,
     ) = ins
-    bo_ref, ig_ref, eg_ref, *dense_refs, small_out = outs
-    x_ref, g_ref, gain1_ref, gain2_ref = scratch["loads"][:4]
+    bo_ref, ig_ref, gain1_out, wqkv_out, wattn_out, gain2_out, router_out = outs[:7]
+    ein_out, eout_out = outs[7:]
+    xin_ref, gin_ref, gain1_ref, gain2_ref = scratch["loads"][:4]
     wqkv_ref, wattn_ref, wrt_ref = scratch["loads"][4:7]
     ids_ref, slot_ref, drop_ref, w1, w2 = scratch["loads"][7:]
-    n1_ref, qkv_ref, p_ref, am_ref, res_ref, n2_ref = scratch["saved"]
-    rs_ref, cols_ref, slope_ref = scratch["work"]
-    act_ref, hg_ref, xg_ref, x1_ref, xs_ref, gacc_ref = scratch["expert"]
+    x_ref, g_ref, n1_ref, qkv_ref, p_ref, am_ref, res_ref, n2_ref = scratch["saved"]
+    rs_ref, cols_ref, slope_ref, pick_ref = scratch["work"]
+    act_ref, hg_ref, xg_ref, x1_ref, xs_ref, eg_ref, gacc_ref = scratch["expert"]
     dq_ref, acc_ref, small_ref, t1_ref, t2_ref, t3_ref = scratch["grads"]
     lsem, esem, xsem, tsem = scratch["sems"]
     chunks = scratch["chunks"]
@@ -141,7 +144,7 @@
     ]
     for n, (src, dst) in enumerate(zip(sources, scratch["loads"])):
         loads.append(pltpu.make_async_copy(src, dst, lsem.at[n]))
-    for n in (0, 2, 4, 5, 3, 6, 7, 8, 9, 1, 10, 11):
+    for n in (0, 2, 4, 7, 8, 9, 1, 5, 3, 6, 10, 11):
         loads[n].start()
 
     def ready(*which):
@@ -184,14 +187,39 @@
         spread = jnp.where(slot_lane, row, 0.0)
         return jnp.sum(spread, axis=-1, keepdims=True).reshape(S, 1)
 
-    def forward(mb):
+    def route(mb):
+        if mb == 0:
+            ready(7, 8, 9, 1)
+        g_ref[mb, TP - 16 : TP] = jnp.zeros((16, D), BF16)
+        g_ref[mb, 0:SEQ] = gin_ref[:, mb, :]
+        ids = ids_ref[mb]
+        drop = drop_ref[mb]
+        slot = slot_ref[mb]
+        flat = jnp.where(drop == 0, ids * CAP + slot, S)
+        rs_ref[mb] = jnp.zeros_like(rs_ref[mb])
+        rs_ref[mb, G : G + 2, 0:TP] = jnp.full((2, TP), S, F32)
+        rs_ref[mb, G : G + 2, 0:SEQ] = flat.astype(F32)
+        rs_ref[mb, G + 2 : G + 4, 0:SEQ] = 1.0 - drop.astype(F32)
+        rs_ref[mb, G + 4 : G + 6, 0:SEQ] = ids.astype(F32)
+        rs_ref[mb, G + 8 : G + 10, 0:SEQ] = slot.astype(F32)
+        slot_of = lax.broadcasted_iota(jnp.int32, (S, TP), 0).astype(F32)
+        hit0 = slot_of == rs_ref[mb, G : G + 1, 0:TP]
+        hit1 = slot_of == rs_ref[mb, G + 1 : G + 2, 0:TP]
+        pick = jnp.where(hit0, 1.0, jnp.where(hit1, 1.0, 0.0)).astype(BF16)
+        pick_ref[mb] = pick
+        scratch["pull"][0][mb] = mm(pick, g_ref[mb]).astype(BF16).reshape(G, CAP, D)
+
+    def project(mb):
         if mb == 0:
             ready(0, 2, 4)
-        x = x_ref[mb].astype(F32)
-        hat, _ = normed_of(x)
+        x_ref[mb, TP - 16 : TP] = jnp.zeros((16, D), F32)
+        x_ref[mb, 0:SEQ] = xin_ref[:, mb, :].astype(F32)
+        hat, _ = normed_of(x_ref[mb])
         n1 = (hat * gain1_ref[...].reshape(1, D)).astype(BF16)
         n1_ref[mb] = n1
         qkv_ref[mb] = mm(n1, wqkv_ref[...]).astype(BF16)
+
+    def forward(mb):
         for pair in range(HEADS // 2):
             c = pair * 128
             q = qkv_ref[mb, :, c : c + 128] * jnp.asarray(HD**-0.5, BF16)
@@ -211,8 +239,8 @@
                 low_half, mixed[0], mixed[1]
             ).astype(BF16)
         if mb == 0:
-            ready(5, 3, 6, 7, 8, 9, 1)
-        res = x + mm(am_ref[mb], wattn_ref[...])
+            ready(5, 3, 6)
+        res = x_ref[mb] + mm(am_ref[mb], wattn_ref[...])
         res_ref[mb] = res
         hat2, _ = normed_of(res)
         n2 = (hat2 * gain2_ref[...].reshape(1, D)).astype(BF16)
@@ -220,36 +248,24 @@
         logits = mm(wrt_ref[...], n2, 1, 1)
         ex = jnp.exp(logits - jnp.max(logits, axis=0, keepdims=True))
         gp = ex / jnp.sum(ex, axis=0, keepdims=True)
-        ids = ids_ref[mb]
-        drop = drop_ref[mb]
-        slot = slot_ref[mb]
-        flat = jnp.where(drop == 0, ids * CAP + slot, S)
-        rs_ref[...] = jnp.zeros_like(rs_ref)
-        rs_ref[0:G, 0:TP] = gp
-        rs_ref[G : G + 2, 0:TP] = jnp.full((2, TP), S, F32)
-        rs_ref[G : G + 2, 0:SEQ] = flat.astype(F32)
-        rs_ref[G + 2 : G + 4, 0:SEQ] = 1.0 - drop.astype(F32)
-        rs_ref[G + 4 : G + 6, 0:SEQ] = ids.astype(F32)
-        rs_ref[G + 8 : G + 10, 0:SEQ] = slot.astype(F32)
+        rs_ref[mb, 0:G, 0:TP] = gp
         expert_of = lax.broadcasted_iota(jnp.int32, (G, TP), 0).astype(F32)
         slot_of = lax.broadcasted_iota(jnp.int32, (S, TP), 0).astype(F32)
-        pick = jnp.zeros((S, TP), F32)
         gcol = jnp.zeros((S, 1), F32)
         for kk in range(2):
-            flr = rs_ref[G + kk : G + kk + 1, 0:TP]
-            keep = rs_ref[G + 2 + kk : G + 3 + kk, 0:TP]
-            idr = rs_ref[G + 4 + kk : G + 5 + kk, 0:TP]
+            flr = rs_ref[mb, G + kk : G + kk + 1, 0:TP]
+            keep = rs_ref[mb, G + 2 + kk : G + 3 + kk, 0:TP]
+            idr = rs_ref[mb, G + 4 + kk : G + 5 + kk, 0:TP]
             mine = jnp.where(expert_of == idr, gp, 0.0)
             gate = jnp.sum(mine, axis=0, keepdims=True) * keep
-            rs_ref[G + 6 + kk : G + 7 + kk, 0:TP] = gate
+            rs_ref[mb, G + 6 + kk : G + 7 + kk, 0:TP] = gate
             hit = slot_of == flr
-            pick = pick + jnp.where(hit, 1.0, 0.0)
             gcol = gcol + jnp.sum(jnp.where(hit, gate, 0.0), axis=-1, keepdims=True)
-        cols_ref[mb] = rs_ref[...].T
-        pick = pick.astype(BF16)
-        scratch["rows"][0][mb] = mm(pick, n2).astype(BF16).reshape(G, CAP, D)
+        scratch["rows"][0][mb] = mm(pick_ref[mb], n2).astype(BF16).reshape(G, CAP, D)
         scratch["gate"][0][mb] = row_of_slots(gcol)
-        scratch["pull"][0][mb] = mm(pick, g_ref[mb]).astype(BF16).reshape(G, CAP, D)
+        exchange("rows", mb)
+        exchange("gate", mb)
+        cols_ref[mb] = rs_ref[mb].T
 
     def experts(mb):
         xs = arrived("rows", mb)[...].reshape(S, D)
@@ -348,24 +364,77 @@
             xs_ref.at[j, mat], eg_ref.at[j, mat], xsem.at[1 + mat, 1]
         ).start()
 
+    def slices_out(mat):
+        wait_bytes(xs_ref.at[pl.ds(0, L), 0], xsem.at[1 + mat, 1])
+        out = (ein_out, eout_out)[mat]
+
+        def part(i, carry):
+            out[i] = eg_ref[i, mat].astype(F32)
+            return carry
+
+        lax.fori_loop(0, L, part, 0)
+
+    def chunk_of(block):
+        for ck in chunks:
+            at = 0
+            for name in ck["blocks"]:
+                if name == block:
+                    return ck, at
+                at += ROWS[name]
+
     def add_block(block, value):
-        for ck in chunks:
-            if block in ck["blocks"]:
-                src, pr = ck["src"], ck["pr"]
-                at = ck["blocks"].index(block) * (D // pr)
+        ck, at = chunk_of(block)
+        src, pr = ck["src"], ck["pr"]
+        at = at // pr
+        count = ROWS[block] // pr
         if pr % 8 == 0:
-            value = value.reshape(D // pr, pr, D)
-            src[at : at + D // pr] = value.astype(BF16)
+            src[at : at + count] = value.reshape(count, pr, D).astype(BF16)
         else:
-            acc_ref[block * D : (block + 1) * D] = value
+            first = START[block]
+            acc_ref[first : first + ROWS[block]] = value
             rows = math.lcm(pr, 8)
 
-            @pl.loop(0, D // rows)
+            @pl.loop(0, ROWS[block] // rows)
             def _(n):
-                first = pl.multiple_of(block * D + n * rows, 8)
-                piece = acc_ref[pl.ds(first, rows)].astype(BF16)
+                piece = acc_ref[pl.ds(pl.multiple_of(first + n * rows, 8), rows)]
+                piece = piece.astype(BF16)
                 for m in range(rows // pr):
                     src[at + n * (rows // pr) + m] = piece[m * pr : (m + 1) * pr]
+
+    def total_of(block):
+        ck, at = chunk_of(block)
+        out, pr = ck["out"], ck["pr"]
+        at = at // pr
+        count = ROWS[block] // pr
+        if pr % 8 == 0:
+            return out[at : at + count].astype(F32).reshape(ROWS[block], D)
+        first = START[block]
+        rows = math.lcm(pr, 8)
+
+        @pl.loop(0, ROWS[block] // rows)
+        def _(n):
+            pieces = [out[at + n * (rows // pr) + m] for m in range(rows // pr)]
+            spot = pl.ds(pl.multiple_of(first + n * rows, 8), rows)
+            acc_ref[spot] = jnp.concatenate(
+                [piece.astype(F32) for piece in pieces], axis=0
+            )
+
+        return acc_ref[first : first + ROWS[block]]
+
+    def store_totals(ck):
+        for block in ck["blocks"]:
+            total = total_of(block)
+            if block == 0:
+                wattn_out[...] = total
+            elif block == 1:
+                wqkv_out[:, 2 * D : 3 * D] = total
+            else:
+                for n in range(2):
+                    c = n * D + (block - 2) * 128
+                    for m in range(3):
+                        wqkv_out[m * 128 : (m + 1) * 128, c : c + 128] = total[
+                            n * 128 : (n + 1) * 128, m * 128 : (m + 1) * 128
+                        ]
 
     def sum_start(ck):
         for n in range(1, L + 1):
@@ -507,7 +576,10 @@
         small_start(level + 1)
 
     def small_end():
-        small_out[...] = small_sum(2)
+        total = small_sum(2)
+        router_out[...] = total[0:G]
+        gain2_out[...] = total[G]
+        gain1_out[...] = total[G + 1]
         for level in range(3):
             buf, _, count, _ = levels[level]
             if count > 1:
@@ -516,7 +588,7 @@
     last = MB - 1
 
     def add_grad(mb, block, value):
-        at = slice(block * D, (block + 1) * D)
+        at = slice(START[block], START[block] + ROWS[block])
         if mb > 0:
             value = value + acc_ref[at]
         if mb < last:
@@ -564,7 +636,7 @@
         gain2 = gain2_ref[...].reshape(1, D)
         rgrad = g + norm_pull(hat2, rstd2, gain2, ngrad)
         branch = rgrad.astype(BF16)
-        add_grad(mb, 3, mm(am_ref[mb], branch, 0, 0))
+        add_grad(mb, 0, mm(am_ref[mb], branch, 0, 0))
         mgrad = mm(branch, wattn_ref[...], 1, 1).astype(BF16)
         for pair in range(HEADS // 2):
             c = pair * 128
@@ -577,8 +649,9 @@
                 low_half, dvs[0], dvs[1]
             ).astype(BF16)
         n1 = n1_ref[mb]
-        add_grad(mb, 2, mm(n1, dq_ref[:, 2 * D : 3 * D], 0, 0))
-        if mb == last and len(chunks) > 1:
+        add_grad(mb, 1, mm(n1, dq_ref[:, 2 * D : 3 * D], 0, 0))
+        piped = mb == last and len(chunks) > 1
+        if piped:
             sum_start(chunks[0])
         for pair in range(HEADS // 2):
             c = pair * 128
@@ -596,23 +669,40 @@
                 ds = (p * (dp_ - delta) * HD**-0.5).astype(BF16)
                 dqs.append(mm(ds, k))
                 dks.append(mm(ds, q, 0, 0))
-            for n, parts in enumerate((dqs, dks)):
-                dq_ref[:, n * D + c : n * D + c + 128] = jnp.where(
-                    low_half, parts[0], parts[1]
-                ).astype(BF16)
-        for n in range(2):
-            add_grad(mb, n, mm(n1, dq_ref[:, n * D : (n + 1) * D], 0, 0))
-        if mb == last:
-            sum_start(chunks[-1])
-            if len(chunks) > 1:
-                sum_pairs(chunks[0])
+            grads = [
+                jnp.where(low_half, parts[0], parts[1]).astype(BF16)
+                for parts in (dqs, dks)
+            ]
+            for n in range(2):
+                dq_ref[:, n * D + c : n * D + c + 128] = grads[n]
+            wgrad = mm(n1, jnp.concatenate(grads, axis=1), 0, 0)
+            packed = jnp.concatenate(
+                [
+                    jnp.concatenate(
+                        [
+                            wgrad[m * 128 : (m + 1) * 128, n * 128 : (n + 1) * 128]
+                            for m in range(3)
+                        ],
+                        axis=1,
+                    )
+                    for n in range(2)
+                ],
+                axis=0,
+            )
+            add_grad(mb, 2 + pair, packed)
+            if piped:
+                sum_start(chunks[1 + pair])
+                sum_pairs(chunks[pair])
+        if mb == last and not piped:
+            sum_start(chunks[0])
         fgrad = mm(dq_ref[...], wqkv_ref[...], 1, 1)
-        hat, rstd = normed_of(x_ref[mb].astype(F32))
+        hat, rstd = normed_of(x_ref[mb])
         add_small(
             mb, slice(G + 1, G + 2), jnp.sum(fgrad * hat, axis=0, keepdims=True)
         )
         gain1 = gain1_ref[...].reshape(1, D)
-        ig_ref[mb] = rgrad + norm_pull(hat, rstd, gain1, fgrad)
+        grad = rgrad + norm_pull(hat, rstd, gain1, fgrad)
+        ig_ref[:, mb, :] = grad[0:SEQ]
 
     def combine(mb):
         _, col = cols_of(mb)
@@ -622,16 +712,18 @@
         for kk in range(2):
             pick = jnp.where(slot_at == col(G + kk), 1.0, 0.0).astype(BF16)
             out = out + col(G + 6 + kk) * mm(pick, made)
-        bo_ref[mb] = out
-
+        bo_ref[:, mb, :] = out[0:SEQ]
+
+    project(0)
+    route(0)
+    pl.semaphore_wait(barrier, G - 1 + R - 1)
+    exchange("pull", 0)
     forward(0)
-    pl.semaphore_wait(barrier, G - 1 + R - 1)
-    for kind in ("rows", "gate", "pull"):
-        exchange(kind, 0)
     for mb in range(1, MB):
+        project(mb)
+        route(mb)
         forward(mb)
-        for kind in ("rows", "gate", "pull"):
-            exchange(kind, mb)
+        exchange("pull", mb)
     ready(10, 11)
     for mb in range(MB):
         experts(mb)
@@ -648,31 +740,29 @@
             hand_out(0)
     t1_ref[r] = small_ref[...].astype(BF16)
     small_start(0)
-    if len(chunks) > 1:
-        sum_plane(chunks[0])
     sum_pairs(chunks[-1])
+    combine(0)
     small_next(0)
-    if len(chunks) > 1:
-        sum_z(chunks[0])
-    combine(0)
-    sum_plane(chunks[-1])
-    small_next(1)
+    for ck in chunks:
+        sum_plane(ck)
     hand_out(1)
-    if len(chunks) > 1:
-        spread_plane(chunks[0])
     for mb in range(1, MB):
         combine(mb)
-    sum_z(chunks[-1])
-    if len(chunks) > 1:
-        spread_parts(chunks[0])
-    spread_plane(chunks[-1])
-    spread_parts(chunks[-1])
+    small_next(1)
+    for ck in chunks:
+        sum_z(ck)
+    slices_out(0)
+    for ck in chunks:
+        spread_plane(ck)
+    slices_out(1)
     small_end()
     for ck in chunks:
+        spread_parts(ck)
+    for ck in chunks:
         sum_end(ck)
+        store_totals(ck)
 
     for mat in range(2):
-        wait_bytes(xs_ref.at[pl.ds(0, L), 0], xsem.at[1 + mat, 1])
         if L > 1:
             wait_bytes(xs_ref.at[pl.ds(0, L - 1), 0], xsem.at[1 + mat, 0])
     if R > 1:
@@ -706,16 +796,17 @@
     S = G * CAP
     FS = FF // replicas
     parts = R * L * Z
-    groups_of_blocks = [(2, 3), (0, 1)]
-    if 2 * D % parts or (2 * D // parts) % 8:
-        groups_of_blocks = [(0, 1, 2, 3)]
+    groups_of_blocks = [(0, 1), (2,), (3,), (4,)]
+    if any(n % (8 * parts) for n in ROWS[2:]):
+        groups_of_blocks = [(0, 1, 2, 3, 4)]
+    rows_of = [sum(ROWS[n] for n in blocks) for blocks in groups_of_blocks]
     small_rows = -(-(G + 2) // SM) * SM
     rs_rows = -(-(G + 10) // 8) * 8
-    pad = ((0, 0), (0, TP - SEQ), (0, 0))
     swap = lambda a: jnp.transpose(a, (0, 2, 1))
+    turn = lambda a: jnp.transpose(a, (1, 0, 2))
     operands = (
-        jnp.pad(inputs, pad),
-        jnp.pad(out_grad, pad),
+        turn(inputs),
+        turn(out_grad),
         first_gain,
         second_gain,
         w_qkv,
@@ -728,7 +819,7 @@
         expert_out,
     )
     vmem = pl.BlockSpec(memory_space=pltpu.VMEM)
-    hbm = pl.BlockSpec(memory_space=pl.ANY)
+    hbm = pl.BlockSpec(memory_space=pltpu.HBM)
     sds = jax.ShapeDtypeStruct
     V = pltpu.VMEM
     dma = pltpu.SemaphoreType.DMA
@@ -736,6 +827,8 @@
         "loads": [V(a.shape, a.dtype) for a in operands[:10]]
         + [V((D, FF), BF16), V((FF, D), BF16)],
         "saved": [
+            V((MB, TP, D), F32),
+            V((MB, TP, D), BF16),
             V((MB, TP, D), BF16),
             V((MB, TP, 3 * D), BF16),
             V((MB, HEADS, TP, TP), F32),
@@ -744,15 +837,17 @@
             V((MB, TP, D), BF16),
         ],
         "work": [
-            V((rs_rows, TL), F32),
+            V((MB, rs_rows, TL), F32),
             V((MB, TL, rs_rows), F32),
             V((S, FF), F32),
+            V((MB, S, TP), BF16),
         ],
         "expert": [
             V((MB, S, FF), BF16),
             V((MB, S, FF), BF16),
             V((R, L, 2, FS, D), BF16),
             V((max(R - 1, 1), L, 2, FS, D), BF16),
+            V((L, 2, FS, D), BF16),
             V((L, 2, FS, D), BF16),
             V((2, L, FF // L, D), F32),
         ],
@@ -772,11 +867,12 @@
         shape = (MB, G, 1, 128) if slim else (MB, G, CAP, D)
         scratch[kind] = [V(shape, F32 if slim else BF16)] * 2
     scratch["chunks"] = []
-    for blocks in groups_of_blocks:
-        pr = len(blocks) * D // parts
+    for rows in rows_of:
+        pr = rows // parts
         scratch["chunks"].append(
             {
                 "src": V((parts, pr, D), BF16),
+                "out": V((parts, pr, D), BF16),
                 "l1": V((max(R - 1, 1), L, Z, pr, D), BF16),
                 "l2s": V((L, Z, pr, D), BF16),
                 "l2": V((max(L - 1, 1), Z, pr, D), BF16),
@@ -789,53 +885,69 @@
             }
         )
     leaves, tree = jax.tree.flatten(scratch)
-    n_in, n_out = len(operands), 4 + len(groups_of_blocks)
+    results = (
+        sds((SEQ, MB, D), F32),
+        sds((SEQ, MB, D), F32),
+        sds((D,), F32),
+        sds((D, 3 * D), F32),
+        sds((D, D), F32),
+        sds((D,), F32),
+        sds((G, D), F32),
+        sds((L, FS, D), F32),
+        sds((L, FS, D), F32),
+    )
+    n_in, n_out = len(operands), len(results)
 
     def body(*refs):
         ins, outs = refs[:n_in], refs[n_in : n_in + n_out]
         held = jax.tree.unflatten(tree, refs[n_in + n_out :])
-        for n, blocks in enumerate(groups_of_blocks):
-            ck = held["chunks"][n]
-            ck["blocks"] = list(blocks)
-            ck["out"] = outs[3 + n]
-            ck["pr"] = len(blocks) * D // parts
+        for ck, blocks, rows in zip(held["chunks"], groups_of_blocks, rows_of):
+            ck["blocks"] = blocks
+            ck["pr"] = rows // parts
         kernel((L, R, Z, G, FF), ins, outs, held)
 
-    bo, ig, eg, *dense, small = pl.pallas_call(
+    held = pl.pallas_call(
         body,
-        out_shape=(
-            sds((MB, TP, D), F32),
-            sds((MB, TP, D), F32),
-            sds((L, 2, FS, D), BF16),
-            *(
-                sds((parts, len(blocks) * D // parts, D), BF16)
-                for blocks in groups_of_blocks
-            ),
-            sds((small_rows, D), F32),
-        ),
+        out_shape=results,
         in_specs=[hbm] * n_in,
         out_specs=[vmem] * n_out,
         scratch_shapes=leaves,
         compiler_params=pltpu.CompilerParams(
-            collective_id=0, has_side_effects=True, vmem_limit_bytes=63 << 20
+            collective_id=0, has_side_effects=True, vmem_limit_bytes=48 << 20
         ),
         name="block",
-    )(*operands)
-    blocks = {}
-    for names, got in zip(groups_of_blocks, dense):
-        got = got.reshape(len(names), D, D).astype(F32)
-        for n, name in enumerate(names):
-            blocks[name] = got[n]
+    )(*(pltpu.with_memory_space_constraint(a, pltpu.HBM) for a in operands))
+
+    def put_out(*refs):
+        ins, outs, sem = refs[:n_out], refs[n_out:-1], refs[-1]
+        copies = [
+            pltpu.make_async_copy(src, dst, sem.at[n])
+            for n, (src, dst) in enumerate(zip(ins, outs))
+        ]
+        for copy in copies:
+            copy.start()
+        for copy in copies:
+            copy.wait()
+
+    bo, ig, gain1, wqkv, wattn, gain2, router, ein, eout = pl.pallas_call(
+        put_out,
+        out_shape=results,
+        in_specs=[vmem] * n_out,
+        out_specs=[hbm] * n_out,
+        scratch_shapes=[dma((n_out,))],
+        compiler_params=pltpu.CompilerParams(vmem_limit_bytes=1 << 20),
+        name="put_out",
+    )(*held)
     return (
-        bo[:, :SEQ],
-        ig[:, :SEQ],
-        small[G + 1],
-        jnp.concatenate([blocks[n] for n in range(3)], axis=1),
-        blocks[3],
-        small[G],
-        small[:G].T,
-        jnp.transpose(eg[:, 0].astype(F32), (0, 2, 1)),
-        eg[:, 1].astype(F32),
+        turn(bo),
+        turn(ig),
+        gain1,
+        wqkv,
+        wattn,
+        gain2,
+        router.T,
+        jnp.transpose(ein, (0, 2, 1)),
+        eout,
     )
 
 

time: 86.4 us -> 73.5 us (0.85)
  local copies, waits for them, and re-layouts: 9.69 us -> 0 us
  other arithmetic: 2.88 us -> 0 us
    unnamed x14 -> x0, local copies, waits for them, and re-layouts: 4.78 us -> none
    slice x4 -> x0, local copies, waits for them, and re-layouts: 2.79 us -> none  [the longest x1 1.18 us: on_device(): bo[:, :SEQ]]
    convert_element_type x1 -> x0, other arithmetic: 1.56 us -> none  [on_device(): eg[:, 1].astype(F32)]
    pad x2 -> x0, local copies, waits for them, and re-layouts: 1.51 us -> none  [the longest x1 0.76 us: on_device(): jnp.pad(inputs, pad)]
    concatenate x1 -> x0, other arithmetic: 1.32 us -> none  [on_device(): jnp.concatenate([blocks[n] for n in range(3)], axis=1)]
    pallas_call x1 -> x2, Pallas kernels: 72.9 us -> 72.5 us  [the longest x1 69.8 us: on_device(): pl.pallas_call(body, out_shape=results, in_specs=[hbm] * n_in, out_specs=...]
where the time goes in v2:
time: 73.5 us; the launch traced here: 73.3 us
  Pallas kernels  72.5 us (99%)
  between operations  0.82 us (1%)
    pallas_call x1, Pallas kernels, on_device(): pl.pallas_call(body, out_shape=results, in_specs=[hbm] * n_in, out_specs=...  69.8 us
    pallas_call x1, Pallas kernels, on_device(): pl.pallas_call(put_out, out_shape=results, in_specs=[vmem] * n_out, out_s...  2.68 us

profile of v2, /device:TPU:0, one launch (start us, length us, event | category | flops | bytes accessed | tf_op | source)
XLA Modules:
  0.0 73.3 jit_solution(6612601725242232743)
XLA Ops:
  0.6 69.8 %block.1 = (f32[197,2,384]{2,1,0:T(2,128)S(1)}, f32[197,2,384]{2,1,0:T(2,128)S(1)}, f32[384]{0:T(512)S(1)}, f32[384,1152]{1,0:T(8,128)S(1)}, f32[384,384]{1,0:T(...) custom-call(bf16[197,2,384]{2,1,0:T(2,128)(2,1)} %bitcast.10, ...), custom_call_target="tpu_custom_call" | custom-call | tf_op jit(solution)/shard_map/block/pallas_call | solution.py:909
  70.5 2.7 %put_out.1 = (f32[197,2,384]{2,1,0:T(2,128)}, f32[197,2,384]{2,1,0:T(2,128)}, f32[384]{0:T(512)}, f32[384,1152]{1,0:T(8,128)}, f32[384,384]{1,0:T(8,128)}, /*ind...) custom-call(f32[197,2,384]{2,1,0:T(2,128)S(1)} %get-tuple-element.27.refs_0_, ...), custom_call_target="tpu_custom_call" | custom-call | tf_op jit(solution)/shard_map/put_out/pallas_call | solution.py:932

commit v3 on v2

--- a/solution.py
+++ b/solution.py
@@ -18,11 +18,16 @@
 TP = 208
 TL = 256
 SM = 32
-ROWS = (D, D, 256, 256, 256)
-START = (0, D, 2 * D, 2 * D + 256, 2 * D + 512)
+ROWS = (256, 128, 128, 256, 256, 256, 256)
+START = (0, 256, 384, 512, 768, 1024, 1280)
+CHUNKS = ((0,), (1, 2), (3,), (4,), (5,), (6,))
 F32 = jnp.float32
 BF16 = jnp.bfloat16
 MESH = pl.DeviceIdType.MESH
+EARLY = 2
+Z_TIMES = ((3.5, 1.5), (7.5, 1.5), (11.0, 1.5), (15.5, 1.2))
+XY_TIMES = ((3.0, 0.9), (8.0, 0.9), (12.0, 0.8), (15.5, 0.8))
+X_TIMES = (7.1, 8.2, 9.1, 10.0)
 KINDS = ("rows", "gate", "pull", "ggrad", "back", "made")
 
 
@@ -83,9 +88,11 @@
     x_ref, g_ref, n1_ref, qkv_ref, p_ref, am_ref, res_ref, n2_ref = scratch["saved"]
     rs_ref, cols_ref, slope_ref, pick_ref = scratch["work"]
     act_ref, hg_ref, xg_ref, x1_ref, xs_ref, eg_ref, gacc_ref = scratch["expert"]
-    dq_ref, acc_ref, small_ref, t1_ref, t2_ref, t3_ref = scratch["grads"]
-    lsem, esem, xsem, tsem = scratch["sems"]
+    dq_ref, held_rgrad, acc_ref, small_ref, t1_ref, t2_ref, t3_ref = scratch["grads"]
+    lsem, esem, xsem, tsem, ssem, x1sem = scratch["sems"]
+    sums_ref = scratch["sums"]
     chunks = scratch["chunks"]
+    last = MB - 1
     dp = lax.axis_index("dp")
     z = lax.axis_index("expert")
     j = dp // R
@@ -113,6 +120,12 @@
 
     def wait_bytes(ref, sem):
         pltpu.make_async_copy(ref, ref, sem).wait()
+
+    for n, ck in enumerate(chunks):
+        ck["src"] = sums_ref.at[pl.ds(n * G * R, G * R)]
+        plane = (j, L, plane_id)
+        along = (z, Z, lambda i: (dp, i))
+        ck["dims"] = (along, plane) if ck["z_first"] else (plane, along)
 
     barrier = pltpu.get_barrier_semaphore()
 
@@ -157,22 +170,29 @@
         jnp.int32, (G, CAP, 128), 2
     ) == lax.broadcasted_iota(jnp.int32, (G, CAP, 128), 1)
 
-    def exchange(kind, mb):
-        send, recv = scratch[kind]
-        send, recv = send.at[mb], recv.at[mb]
-        n = KINDS.index(kind)
-        pltpu.make_async_copy(send.at[me], recv.at[me], esem.at[n, mb, 1]).start()
+    def exchange(*which):
+        legs = []
+        for kind, mb in which:
+            send, recv = scratch[kind]
+            sems = esem.at[KINDS.index(kind), mb]
+            legs.append((send.at[mb], recv.at[mb], sems))
+        for send, recv, sems in legs:
+            pltpu.make_async_copy(send.at[me], recv.at[me], sems.at[1]).start()
 
         @pl.loop(1, G)
         def _(o):
             e = (me + o) % G
-            remote(
-                send.at[e],
-                recv.at[me],
-                esem.at[n, mb, 0],
-                esem.at[n, mb, 1],
-                group_id(e),
-            )
+            to = group_id(e)
+            for send, recv, sems in legs:
+                remote(send.at[e], recv.at[me], sems.at[0], sems.at[1], to)
+
+    def for_core(core, what):
+        pl.when(dp % 2 == core)(what)
+
+    def left(*which):
+        for kind, mb in which:
+            sent = scratch[kind][0].at[mb, pl.ds(0, G - 1)]
+            wait_bytes(sent, esem.at[KINDS.index(kind), mb, 0])
 
     def arrived(kind, mb):
         recv = scratch[kind][1].at[mb]
@@ -263,12 +283,12 @@
             gcol = gcol + jnp.sum(jnp.where(hit, gate, 0.0), axis=-1, keepdims=True)
         scratch["rows"][0][mb] = mm(pick_ref[mb], n2).astype(BF16).reshape(G, CAP, D)
         scratch["gate"][0][mb] = row_of_slots(gcol)
-        exchange("rows", mb)
-        exchange("gate", mb)
         cols_ref[mb] = rs_ref[mb].T
 
-    def experts(mb):
-        xs = arrived("rows", mb)[...].reshape(S, D)
+    def experts(mb, halfway=None):
+        if mb == last:
+            arrived("rows", mb)
+        xs = scratch["rows"][1][mb].reshape(S, D)
         step = 384
         produced = jnp.zeros((S, D), F32)
         for c in range(0, FF, step):
@@ -284,6 +304,8 @@
             produced = produced + mm(act, w2[c : c + step, :])
         produced = produced.astype(BF16)
         scratch["made"][0][mb] = produced.reshape(G, CAP, D)
+        if halfway is not None:
+            halfway()
         gates = slots_of_row(arrived("gate", mb)[...])
         grow = arrived("pull", mb)[...].reshape(S, D).astype(F32)
         pg = (gates * grow).astype(BF16)
@@ -297,71 +319,70 @@
             hg_ref[mb, :, c : c + step] = hg
             back = back + mm(hg, w1[:, c : c + step], 1, 1)
         scratch["back"][0][mb] = back.astype(BF16).reshape(G, CAP, D)
-        exchange("ggrad", mb)
-        exchange("back", mb)
 
     span = FF // L
 
-    def weight_grads(mb):
+    def weight_grads(mb, mats):
         xs = scratch["rows"][1][mb].reshape(S, D)
         pg = scratch["gated"][mb]
 
         def part(i, carry):
             at = pl.ds(pl.multiple_of(i * span, 128), span)
-            g1 = mm(hg_ref[mb, :, at], xs, 0, 0)
-            g2 = mm(act_ref[mb, :, at], pg, 0, 0)
-            if mb < MB - 1:
+            for mat in mats:
+                left_rows = (hg_ref, act_ref)[mat][mb, :, at]
+                grad = mm(left_rows, (xs, pg)[mat], 0, 0)
                 if mb > 0:
-                    g1 = g1 + gacc_ref[0, i]
-                    g2 = g2 + gacc_ref[1, i]
-                gacc_ref[0, i] = g1
-                gacc_ref[1, i] = g2
-            else:
-                g1 = (g1 + gacc_ref[0, i]).astype(BF16)
-                g2 = (g2 + gacc_ref[1, i]).astype(BF16)
-                for rr in range(R):
-                    xg_ref[rr, i, 0] = g1[rr * FS : (rr + 1) * FS]
-                    xg_ref[rr, i, 1] = g2[rr * FS : (rr + 1) * FS]
+                    grad = grad + gacc_ref[mat, i]
+                if mb < last:
+                    gacc_ref[mat, i] = grad
+                else:
+                    grad = grad.astype(BF16)
+                    for rr in range(R):
+                        xg_ref[mat, rr, i] = grad[rr * FS : (rr + 1) * FS]
             return carry
 
         lax.fori_loop(0, L, part, 0)
 
-    def swap_slices():
+    def swap_slices(mat):
         for o in range(1, R):
             rr = (r + o) % R
             remote(
-                xg_ref.at[rr],
-                x1_ref.at[R - o - 1],
-                xsem.at[0, 0],
-                xsem.at[0, 1],
+                xg_ref.at[mat, rr],
+                x1_ref.at[mat, R - o - 1],
+                x1sem.at[mat, 0],
+                x1sem.at[mat, 1],
                 part_id(rr),
             )
 
-    def add_slices():
+    def add_slices(mat):
         if R > 1:
-            wait_bytes(x1_ref, xsem.at[0, 1])
+            wait_bytes(x1_ref.at[mat], x1sem.at[mat, 1])
 
         def part(i, carry):
-            total = xg_ref[r, i].astype(F32)
+            total = xg_ref[mat, r, i].astype(F32)
             for o in range(R - 1):
-                total = total + x1_ref[o, i].astype(F32)
-            xs_ref[i] = total.astype(BF16)
+                total = total + x1_ref[mat, o, i].astype(F32)
+            xs_ref[i, mat] = total.astype(BF16)
             return carry
 
         lax.fori_loop(0, L, part, 0)
 
-    def hand_out(mat):
+    pieces = max(1, FS // 48)
+
+    def hand_out(which):
+        mat, piece = which
+        rows = pl.ds(piece * (FS // pieces), FS // pieces)
         for o in range(1, L):
             i = (j + o) % L
             remote(
-                xs_ref.at[i, mat],
-                eg_ref.at[j, mat],
+                xs_ref.at[i, mat, rows],
+                eg_ref.at[j, mat, rows],
                 xsem.at[1 + mat, 0],
                 xsem.at[1 + mat, 1],
                 plane_id(i),
             )
         pltpu.make_async_copy(
-            xs_ref.at[j, mat], eg_ref.at[j, mat], xsem.at[1 + mat, 1]
+            xs_ref.at[j, mat, rows], eg_ref.at[j, mat, rows], xsem.at[1 + mat, 1]
         ).start()
 
     def slices_out(mat):
@@ -422,129 +443,132 @@
         return acc_ref[first : first + ROWS[block]]
 
     def store_totals(ck):
+        if R > 1:
+            wait_bytes(ck["l1"], ck["recv"].at[5])
         for block in ck["blocks"]:
             total = total_of(block)
-            if block == 0:
-                wattn_out[...] = total
-            elif block == 1:
-                wqkv_out[:, 2 * D : 3 * D] = total
+            if block < 2:
+                wattn_out[START[block] : START[block] + ROWS[block]] = total
+            elif block < 4:
+                first = START[block] - D
+                wqkv_out[first : first + ROWS[block], 2 * D : 3 * D] = total
             else:
                 for n in range(2):
-                    c = n * D + (block - 2) * 128
+                    c = n * D + (block - 4) * 128
                     for m in range(3):
                         wqkv_out[m * 128 : (m + 1) * 128, c : c + 128] = total[
                             n * 128 : (n + 1) * 128, m * 128 : (m + 1) * 128
                         ]
 
     def sum_start(ck):
-        for n in range(1, L + 1):
-            i = (j + n) % L
-            for o in range(1, R):
-                rr = (r + o) % R
-                remote(
-                    ck["src"].at[pl.ds((rr * L + i) * Z, Z)],
-                    ck["l1"].at[R - o - 1, i],
-                    ck["send"].at[0],
-                    ck["s1"].at[R - o - 1, i],
-                    part_id(rr),
-                )
+        (_, A, _), (_, B, _) = ck["dims"]
+        for o in range(1, R):
+            rr = (r + o) % R
+            remote(
+                ck["src"].at[pl.ds(rr * A * B, A * B)],
+                ck["l1"].at[R - o - 1],
+                ssem.at[0],
+                ck["recv"].at[0],
+                part_id(rr),
+            )
 
     def sum_pairs(ck):
-        for n in range(1, L + 1):
-            i = (j + n) % L
-            total = ck["src"][pl.ds((r * L + i) * Z, Z)].astype(F32)
+        (a, A, ident), (_, B, _) = ck["dims"]
+        if R > 1:
+            wait_bytes(ck["l1"], ck["recv"].at[0])
+        for n in range(1, A + 1):
+            i = (a + n) % A
+            total = ck["src"][pl.ds((r * A + i) * B, B)].astype(F32)
             for o in range(R - 1):
-                wait_bytes(ck["l1"].at[o, i], ck["s1"].at[o, i])
-                total = total + ck["l1"][o, i].astype(F32)
+                total = total + ck["l1"][o, pl.ds(i * B, B)].astype(F32)
             ck["l2s"][i] = total.astype(BF16)
-            if n < L:
+            if n < A:
                 remote(
                     ck["l2s"].at[i],
-                    ck["l2"].at[L - n - 1],
-                    ck["send"].at[1],
+                    ck["l2"].at[A - n - 1],
+                    ssem.at[0],
                     ck["recv"].at[1],
-                    plane_id(i),
+                    ident(i),
                 )
 
-    def sum_plane(ck):
-        if L > 1:
+    def sum_first(ck):
+        (a, A, _), (b, B, ident) = ck["dims"]
+        if A > 1:
             wait_bytes(ck["l2"], ck["recv"].at[1])
-        for n in range(Z - 1, -1, -1):
-            zz = (z + n) % Z
-            total = ck["l2s"][j, zz].astype(F32)
-            for o in range(L - 1):
-                total = total + ck["l2"][o, zz].astype(F32)
-            ck["l3s"][zz] = total.astype(BF16)
+        for n in range(B - 1, -1, -1):
+            i = (b + n) % B
+            total = ck["l2s"][a, i].astype(F32)
+            for o in range(A - 1):
+                total = total + ck["l2"][o, i].astype(F32)
+            ck["l3s"][i] = total.astype(BF16)
             if n > 0:
                 remote(
-                    ck["l3s"].at[zz],
-                    ck["l3"].at[Z - n - 1],
-                    ck["send"].at[2],
+                    ck["l3s"].at[i],
+                    ck["l3"].at[B - n - 1],
+                    ssem.at[1],
                     ck["recv"].at[2],
-                    (dp, zz),
+                    ident(i),
                 )
 
-    def sum_z(ck):
+    def sum_second(ck):
+        (a, A, _), (b, B, ident) = ck["dims"]
         out = ck["out"]
-        if Z > 1:
+        if B > 1:
             wait_bytes(ck["l3"], ck["recv"].at[2])
-        total = ck["l3s"][z].astype(F32)
-        for o in range(Z - 1):
+        total = ck["l3s"][b].astype(F32)
+        for o in range(B - 1):
             total = total + ck["l3"][o].astype(F32)
-        mine = (r * L + j) * Z + z
+        mine = (r * A + a) * B + b
         out[mine] = total.astype(BF16)
-        for n in range(Z - 1, 0, -1):
+        for n in range(B - 1, 0, -1):
             remote(
                 out.at[mine],
                 out.at[mine],
-                ck["send"].at[3],
+                ssem.at[1],
                 ck["recv"].at[3],
-                (dp, (z + n) % Z),
+                ident((b + n) % B),
             )
 
-    def spread_plane(ck):
+    def spread_first(ck):
+        (a, A, ident), (_, B, _) = ck["dims"]
         out = ck["out"]
-        if Z > 1:
+        if B > 1:
             wait_bytes(ck["l3"], ck["recv"].at[3])
-        mine = pl.ds((r * L + j) * Z, Z)
-        for n in range(1, L):
+        mine = pl.ds((r * A + a) * B, B)
+        for n in range(1, A):
             remote(
                 out.at[mine],
                 out.at[mine],
-                ck["send"].at[4],
-                ck["s2"].at[L - n - 1],
-                plane_id((j + n) % L),
+                ssem.at[1],
+                ck["recv"].at[4],
+                ident((a + n) % A),
             )
-        spread_part(ck, j)
-
-    def spread_part(ck, i):
+
+    def spread_parts(ck):
+        (_, A, _), (_, B, _) = ck["dims"]
         out = ck["out"]
-        at = pl.ds((r * L + i) * Z, Z)
+        if A > 1:
+            wait_bytes(ck["l2"], ck["recv"].at[4])
+        mine = pl.ds(r * A * B, A * B)
         for o in range(1, R):
             remote(
-                out.at[at],
-                out.at[at],
-                ck["send"].at[5],
+                out.at[mine],
+                out.at[mine],
+                ssem.at[2],
                 ck["recv"].at[5],
                 part_id((r + o) % R),
             )
 
-    def spread_parts(ck):
-        for n in range(1, L):
-            wait_bytes(ck["l2"].at[n - 1], ck["s2"].at[n - 1])
-            spread_part(ck, (j + n) % L)
-
-    def sum_end(ck):
-        if R > 1:
-            wait_bytes(ck["l1"], ck["recv"].at[5])
-            wait_bytes(ck["l1"], ck["send"].at[0])
-            wait_bytes(ck["l1"], ck["send"].at[5])
-        if L > 1:
-            wait_bytes(ck["l2"], ck["send"].at[1])
-            wait_bytes(ck["l2"], ck["send"].at[4])
-        if Z > 1:
-            wait_bytes(ck["l3"], ck["send"].at[2])
-            wait_bytes(ck["l3"], ck["send"].at[3])
+    def sums_left():
+        counts = [0, 0, 0]
+        for ck in chunks:
+            (_, A, _), (_, B, _) = ck["dims"]
+            counts[0] += (R - 1) * A * B + (A - 1) * B
+            counts[1] += 2 * (B - 1) + (A - 1) * B
+            counts[2] += (R - 1) * A * B
+        for n, total in enumerate(counts):
+            if total:
+                wait_bytes(sums_ref.at[pl.ds(0, total)], ssem.at[n])
 
     levels = ((t1_ref, r, R, part_id), (t2_ref, j, L, plane_id), (t3_ref, z, Z, None))
 
@@ -585,8 +609,6 @@
             if count > 1:
                 wait_bytes(buf.at[pl.ds(0, count - 1)], tsem.at[level, 0])
 
-    last = MB - 1
-
     def add_grad(mb, block, value):
         at = slice(START[block], START[block] + ROWS[block])
         if mb > 0:
@@ -597,7 +619,7 @@
             add_block(block, value)
 
     def add_small(mb, at, value):
-        small_ref[at] = value if mb == 0 else small_ref[at] + value
+        small_ref[at] += value
 
     def cols_of(mb):
         cols = cols_ref[mb][0:TP]
@@ -636,7 +658,16 @@
         gain2 = gain2_ref[...].reshape(1, D)
         rgrad = g + norm_pull(hat2, rstd2, gain2, ngrad)
         branch = rgrad.astype(BF16)
-        add_grad(mb, 0, mm(am_ref[mb], branch, 0, 0))
+        piped = mb == last and len(chunks) > 1
+        wgrad = mm(am_ref[mb], branch, 0, 0)
+        add_grad(mb, 0, wgrad[0:256])
+        add_grad(mb, 1, wgrad[256:D])
+        if piped:
+            sum_start(chunks[0])
+        if mb == last - 1:
+            add_slices(0)
+            for piece in range(pieces):
+                hand_out((0, piece))
         mgrad = mm(branch, wattn_ref[...], 1, 1).astype(BF16)
         for pair in range(HEADS // 2):
             c = pair * 128
@@ -645,14 +676,17 @@
                 mm(p_ref[mb, 2 * pair + half].astype(BF16), mg, 0, 0)
                 for half in range(2)
             ]
-            dq_ref[:, 2 * D + c : 2 * D + c + 128] = jnp.where(
+            dq_ref[mb, :, 2 * D + c : 2 * D + c + 128] = jnp.where(
                 low_half, dvs[0], dvs[1]
             ).astype(BF16)
         n1 = n1_ref[mb]
-        add_grad(mb, 1, mm(n1, dq_ref[:, 2 * D : 3 * D], 0, 0))
-        piped = mb == last and len(chunks) > 1
+        wgrad = mm(n1, dq_ref[mb, :, 2 * D : 3 * D], 0, 0)
+        add_grad(mb, 2, wgrad[0:128])
+        add_grad(mb, 3, wgrad[128:D])
         if piped:
-            sum_start(chunks[0])
+            sum_start(chunks[1])
+            sum_start(chunks[2])
+            sum_pairs(chunks[0])
         for pair in range(HEADS // 2):
             c = pair * 128
             q = qkv_ref[mb, :, c : c + 128]
@@ -674,7 +708,7 @@
                 for parts in (dqs, dks)
             ]
             for n in range(2):
-                dq_ref[:, n * D + c : n * D + c + 128] = grads[n]
+                dq_ref[mb, :, n * D + c : n * D + c + 128] = grads[n]
             wgrad = mm(n1, jnp.concatenate(grads, axis=1), 0, 0)
             packed = jnp.concatenate(
                 [
@@ -689,19 +723,22 @@
                 ],
                 axis=0,
             )
-            add_grad(mb, 2 + pair, packed)
+            add_grad(mb, 4 + pair, packed)
             if piped:
-                sum_start(chunks[1 + pair])
-                sum_pairs(chunks[pair])
+                sum_start(chunks[3 + pair])
+                sum_pairs(chunks[1 + pair])
         if mb == last and not piped:
             sum_start(chunks[0])
-        fgrad = mm(dq_ref[...], wqkv_ref[...], 1, 1)
+        held_rgrad[mb] = rgrad
+
+    def finish(mb):
+        fgrad = mm(dq_ref[mb], wqkv_ref[...], 1, 1)
         hat, rstd = normed_of(x_ref[mb])
         add_small(
             mb, slice(G + 1, G + 2), jnp.sum(fgrad * hat, axis=0, keepdims=True)
         )
         gain1 = gain1_ref[...].reshape(1, D)
-        grad = rgrad + norm_pull(hat, rstd, gain1, fgrad)
+        grad = held_rgrad[mb] + norm_pull(hat, rstd, gain1, fgrad)
         ig_ref[:, mb, :] = grad[0:SEQ]
 
     def combine(mb):
@@ -717,60 +754,85 @@
     project(0)
     route(0)
     pl.semaphore_wait(barrier, G - 1 + R - 1)
-    exchange("pull", 0)
+    exchange(("pull", 0))
     forward(0)
+    exchange(("rows", 0), ("gate", 0))
     for mb in range(1, MB):
         project(mb)
         route(mb)
         forward(mb)
-        exchange("pull", mb)
+        for_core(0, lambda: exchange(("rows", mb), ("gate", mb)))
+        arrived("rows", mb - 1)
+        for_core(1, lambda: exchange(("rows", mb), ("gate", mb)))
+        for_core(0, lambda: exchange(("pull", mb)))
     ready(10, 11)
-    for mb in range(MB):
-        experts(mb)
-        if mb == last:
-            for m in range(MB):
-                exchange("made", m)
-        weight_grads(mb)
-    swap_slices()
+    experts(0)
+    for_core(1, lambda: exchange(("pull", last)))
+    exchange(("ggrad", 0))
+    weight_grads(0, (0, 1))
+    for_core(0, lambda: exchange(("back", 0)))
+    for mb in range(1, MB):
+        experts(mb, lambda: for_core(1, lambda: exchange(("back", mb - 1))))
+        exchange(("ggrad", mb))
+        exchange(("back", mb))
+        weight_grads(mb, (0,))
+    swap_slices(0)
+    exchange(*(("made", mb) for mb in range(last)))
     small_ref[...] = jnp.zeros_like(small_ref)
     for mb in range(MB):
         backward(mb)
-        if mb == 0:
-            add_slices()
-            hand_out(0)
-    t1_ref[r] = small_ref[...].astype(BF16)
-    small_start(0)
-    sum_pairs(chunks[-1])
-    combine(0)
-    small_next(0)
-    for ck in chunks:
-        sum_plane(ck)
-    hand_out(1)
+
+    def late_slices():
+        weight_grads(last, (1,))
+        swap_slices(1)
+
+    def small_begin():
+        t1_ref[r] = small_ref[...].astype(BF16)
+        small_start(0)
+
+    plan = []
+    count = len(chunks)
+    early = sum(ck["z_first"] for ck in chunks)
+    for n, ck in enumerate(chunks):
+        if n >= count - 2 or count == 1:
+            plan.append((0.1 * (n - count), sum_pairs, ck))
+        if ck["z_first"]:
+            times = [t + s * n for t, s in Z_TIMES]
+        else:
+            times = [t + s * (n - early) for t, s in XY_TIMES]
+        steps = (sum_first, sum_second, spread_first, spread_parts)
+        plan.extend((when, step, ck) for when, step in zip(times, steps))
+        plan.append((times[3] + 1.2, store_totals, ck))
+    for piece in range(pieces):
+        plan.append((X_TIMES[piece % 4], hand_out, (1, piece)))
+    plan.append((-0.15, finish, last))
+    plan.append((0.2, lambda _: late_slices(), 0))
+    for mb in range(last):
+        plan.append((0.5, finish, mb))
+    plan.append((0.6, lambda _: small_begin(), 0))
+    plan.append((0.5, lambda _: exchange(("made", last)), 0))
+    plan.append((4.9, add_slices, 1))
+    plan.append((3.0, combine, 0))
+    plan.append((2.7, small_next, 0))
     for mb in range(1, MB):
-        combine(mb)
-    small_next(1)
-    for ck in chunks:
-        sum_z(ck)
-    slices_out(0)
-    for ck in chunks:
-        spread_plane(ck)
-    slices_out(1)
-    small_end()
-    for ck in chunks:
-        spread_parts(ck)
-    for ck in chunks:
-        sum_end(ck)
-        store_totals(ck)
+        plan.append((10.0, combine, mb))
+    plan.append((6.0, small_next, 1))
+    plan.append((9.2, slices_out, 0))
+    plan.append((17.0, slices_out, 1))
+    plan.append((17.1, lambda _: small_end(), 0))
+    for when, what, which in sorted(plan, key=lambda step: step[0]):
+        what(which)
+    sums_left()
 
     for mat in range(2):
         if L > 1:
             wait_bytes(xs_ref.at[pl.ds(0, L - 1), 0], xsem.at[1 + mat, 0])
-    if R > 1:
-        wait_bytes(x1_ref, xsem.at[0, 0])
-    for n, kind in enumerate(KINDS):
-        for mb in range(MB):
-            sent = scratch[kind][0].at[mb, pl.ds(0, G - 1)]
-            wait_bytes(sent, esem.at[n, mb, 0])
+        if R > 1:
+            wait_bytes(x1_ref.at[mat], x1sem.at[mat, 0])
+    for mb in range(MB):
+        left(("rows", mb), ("gate", mb), ("ggrad", mb), ("made", mb))
+        left(("back", mb))
+    left(*(("pull", mb) for mb in range(MB)))
 
 
 def on_device(
@@ -796,17 +858,17 @@
     S = G * CAP
     FS = FF // replicas
     parts = R * L * Z
-    groups_of_blocks = [(0, 1), (2,), (3,), (4,)]
-    if any(n % (8 * parts) for n in ROWS[2:]):
-        groups_of_blocks = [(0, 1, 2, 3, 4)]
+    groups_of_blocks = CHUNKS
+    if any(sum(ROWS[n] for n in blocks) % (8 * parts) for blocks in CHUNKS):
+        groups_of_blocks = [tuple(range(len(ROWS)))]
     rows_of = [sum(ROWS[n] for n in blocks) for blocks in groups_of_blocks]
     small_rows = -(-(G + 2) // SM) * SM
     rs_rows = -(-(G + 10) // 8) * 8
     swap = lambda a: jnp.transpose(a, (0, 2, 1))
-    turn = lambda a: jnp.transpose(a, (1, 0, 2))
+    stored = lambda a: jnp.transpose(a, (1, 0, 2))
     operands = (
-        turn(inputs),
-        turn(out_grad),
+        stored(inputs),
+        stored(out_grad),
         first_gain,
         second_gain,
         w_qkv,
@@ -845,14 +907,15 @@
         "expert": [
             V((MB, S, FF), BF16),
             V((MB, S, FF), BF16),
-            V((R, L, 2, FS, D), BF16),
-            V((max(R - 1, 1), L, 2, FS, D), BF16),
+            V((2, R, L, FS, D), BF16),
+            V((2, max(R - 1, 1), L, FS, D), BF16),
             V((L, 2, FS, D), BF16),
             V((L, 2, FS, D), BF16),
             V((2, L, FF // L, D), F32),
         ],
         "grads": [
-            V((TP, 3 * D), BF16),
+            V((MB, TP, 3 * D), BF16),
+            V((MB, TP, D), F32),
             V((4 * D, D), F32),
             V((small_rows, D), F32),
             V((R, small_rows, D), BF16),
@@ -860,27 +923,26 @@
             V((Z, small_rows, D), BF16),
         ],
         "gated": V((MB, S, D), BF16),
-        "sems": [dma((12,)), dma((len(KINDS), MB, 2)), dma((3, 2)), dma((3, 2))],
+        "sums": V((2 * parts * len(rows_of), rows_of[0] // parts, D), BF16),
+        "sems": [dma((12,)), dma((len(KINDS), MB, 2)), dma((3, 2)), dma((3, 2)), dma((3,)), dma((2, 2))],
     }
     for kind in KINDS:
         slim = kind in ("gate", "ggrad")
         shape = (MB, G, 1, 128) if slim else (MB, G, CAP, D)
         scratch[kind] = [V(shape, F32 if slim else BF16)] * 2
     scratch["chunks"] = []
-    for rows in rows_of:
+    early = EARLY if len(rows_of) > 1 else 0
+    for n, rows in enumerate(rows_of):
         pr = rows // parts
+        A, B = (Z, L) if n < early else (L, Z)
         scratch["chunks"].append(
             {
-                "src": V((parts, pr, D), BF16),
                 "out": V((parts, pr, D), BF16),
-                "l1": V((max(R - 1, 1), L, Z, pr, D), BF16),
-                "l2s": V((L, Z, pr, D), BF16),
-                "l2": V((max(L - 1, 1), Z, pr, D), BF16),
-                "l3s": V((Z, pr, D), BF16),
-                "l3": V((max(Z - 1, 1), pr, D), BF16),
-                "s1": dma((max(R - 1, 1), L)),
-                "s2": dma((max(L - 1, 1),)),
-                "send": dma((6,)),
+                "l1": V((max(R - 1, 1), A * B, pr, D), BF16),
+                "l2s": V((A, B, pr, D), BF16),
+                "l2": V((max(A - 1, 1), B, pr, D), BF16),
+                "l3s": V((B, pr, D), BF16),
+                "l3": V((max(B - 1, 1), pr, D), BF16),
                 "recv": dma((6,)),
             }
         )
@@ -904,6 +966,7 @@
         for ck, blocks, rows in zip(held["chunks"], groups_of_blocks, rows_of):
             ck["blocks"] = blocks
             ck["pr"] = rows // parts
+            ck["z_first"] = len(rows_of) > 1 and blocks in groups_of_blocks[:early]
         kernel((L, R, Z, G, FF), ins, outs, held)
 
     held = pl.pallas_call(
@@ -913,7 +976,7 @@
         out_specs=[vmem] * n_out,
         scratch_shapes=leaves,
         compiler_params=pltpu.CompilerParams(
-            collective_id=0, has_side_effects=True, vmem_limit_bytes=48 << 20
+            collective_id=0, has_side_effects=True, vmem_limit_bytes=53 << 20
         ),
         name="block",
     )(*(pltpu.with_memory_space_constraint(a, pltpu.HBM) for a in operands))
@@ -939,8 +1002,8 @@
         name="put_out",
     )(*held)
     return (
-        turn(bo),
-        turn(ig),
+        stored(bo),
+        stored(ig),
         gain1,
         wqkv,
         wattn,

time: 73.5 us -> 77.1 us (1.049)
  local copies, waits for them, and re-layouts: 0 us -> 6.15 us
  Pallas kernels: 72.5 us -> 69.8 us
    unnamed x0 -> x10, local copies, waits for them, and re-layouts: none -> 6.15 us
    pallas_call x1, Pallas kernels: 69.8 us -> 67.1 us  [on_device(): pl.pallas_call(body, out_shape=results, in_specs=[hbm] * n_in, out_specs=...]
where the time goes in v3:
time: 77.1 us; the launch traced here: 76.8 us
  Pallas kernels  69.8 us (91%)
  local copies, waits for them, and re-layouts  6.15 us (8%)
  between operations  0.83 us (1%)
    pallas_call x1, Pallas kernels, on_device(): pl.pallas_call(body, out_shape=results, in_specs=[hbm] * n_in, out_specs=...  67.1 us
    unnamed x10, local copies, waits for them, and re-layouts  6.15 us
    pallas_call x1, Pallas kernels, on_device(): pl.pallas_call(put_out, out_shape=results, in_specs=[vmem] * n_out, out_s...  2.67 us

profile of v3, /device:TPU:0, one launch (start us, length us, event | category | flops | bytes accessed | tf_op | source)
XLA Modules:
  0.0 76.8 jit_solution(13277185983897529589)
XLA Ops:
  0.6 67.1 %block.1 = (f32[197,2,384]{2,1,0:T(2,128)}, f32[197,2,384]{2,1,0:T(2,128)}, f32[384]{0:T(512)S(1)}, f32[384,1152]{1,0:T(8,128)}, f32[384,384]{1,0:T(8,128)S(1)},...) custom-call(bf16[197,2,384]{2,1,0:T(2,128)(2,1)} %bitcast.10, ...), custom_call_target="tpu_custom_call" | custom-call | tf_op jit(solution)/shard_map/block/pallas_call | solution.py:972
  67.8 0.0 copy-start
  67.8 1.5 %copy-done = f32[384,1152]{1,0:T(8,128)S(1)} copy-done((f32[384,1152]{1,0:T(8,128)S(1)}, f32[384,1152]{1,0:T(8,128)}, u32[]{:S(2)}) %copy-start) | copy-done | bytes 1769496
  69.3 0.0 copy-start.1
  69.3 1.3 %copy-done.1 = f32[4,192,384]{2,1,0:T(8,128)S(1)} copy-done((f32[4,192,384]{2,1,0:T(8,128)S(1)}, f32[4,192,384]{2,1,0:T(8,128)}, u32[]{:S(2)}) %copy-start.1) | copy-done | bytes 1179672
  70.5 0.0 copy-start.2
  70.5 1.3 %copy-done.2 = f32[4,192,384]{2,1,0:T(8,128)S(1)} copy-done((f32[4,192,384]{2,1,0:T(8,128)S(1)}, f32[4,192,384]{2,1,0:T(8,128)}, u32[]{:S(2)}) %copy-start.2) | copy-done | bytes 1179672
  71.8 0.0 copy-start.3
  71.8 1.1 %copy-done.3 = f32[197,2,384]{2,1,0:T(2,128)S(1)} copy-done((f32[197,2,384]{2,1,0:T(2,128)S(1)}, f32[197,2,384]{2,1,0:T(2,128)}, u32[]{:S(2)}) %copy-start.3) | copy-done | bytes 605208
  72.9 0.0 copy-start.4
  72.9 1.1 %copy-done.4 = f32[197,2,384]{2,1,0:T(2,128)S(1)} copy-done((f32[197,2,384]{2,1,0:T(2,128)S(1)}, f32[197,2,384]{2,1,0:T(2,128)}, u32[]{:S(2)}) %copy-start.4) | copy-done | bytes 605208
  74.0 2.7 %put_out.1 = (f32[197,2,384]{2,1,0:T(2,128)}, f32[197,2,384]{2,1,0:T(2,128)}, f32[384]{0:T(512)}, f32[384,1152]{1,0:T(8,128)}, f32[384,384]{1,0:T(8,128)}, /*ind...) custom-call(f32[197,2,384]{2,1,0:T(2,128)S(1)} %copy-done.3, ...), custom_call_target="tpu_custom_call" | custom-call | tf_op jit(solution)/shard_map/put_out/pallas_call | solution.py:995
Async XLA Ops:
  67.8 1.5 %copy-start = (f32[384,1152]{1,0:T(8,128)S(1)}, f32[384,1152]{1,0:T(8,128)}, u32[]{:S(2)}) copy-start(f32[384,1152]{1,0:T(8,128)} %get-tuple-element.30.refs_3_) | copy-start | bytes 5308420
  69.3 1.3 %copy-start.1 = (f32[4,192,384]{2,1,0:T(8,128)S(1)}, f32[4,192,384]{2,1,0:T(8,128)}, u32[]{:S(2)}) copy-start(f32[4,192,384]{2,1,0:T(8,128)} %get-tuple-element.34.refs_7_) | copy-start | bytes 3538948
  70.5 1.3 %copy-start.2 = (f32[4,192,384]{2,1,0:T(8,128)S(1)}, f32[4,192,384]{2,1,0:T(8,128)}, u32[]{:S(2)}) copy-start(f32[4,192,384]{2,1,0:T(8,128)} %get-tuple-element.35.refs_8_) | copy-start | bytes 3538948
  71.8 1.1 %copy-start.3 = (f32[197,2,384]{2,1,0:T(2,128)S(1)}, f32[197,2,384]{2,1,0:T(2,128)}, u32[]{:S(2)}) copy-start(f32[197,2,384]{2,1,0:T(2,128)} %get-tuple-element.27.refs_0_) | copy-start | bytes 1815556
  72.9 1.1 %copy-start.4 = (f32[197,2,384]{2,1,0:T(2,128)S(1)}, f32[197,2,384]{2,1,0:T(2,128)}, u32[]{:S(2)}) copy-start(f32[197,2,384]{2,1,0:T(2,128)} %get-tuple-element.28.refs_1_) | copy-start | bytes 1815556

commit v4 on v3

--- a/solution.py
+++ b/solution.py
@@ -923,7 +923,7 @@
             V((Z, small_rows, D), BF16),
         ],
         "gated": V((MB, S, D), BF16),
-        "sums": V((2 * parts * len(rows_of), rows_of[0] // parts, D), BF16),
+        "sums": V((parts * len(rows_of), rows_of[0] // parts, D), BF16),
         "sems": [dma((12,)), dma((len(KINDS), MB, 2)), dma((3, 2)), dma((3, 2)), dma((3,)), dma((2, 2))],
     }
     for kind in KINDS:
@@ -976,7 +976,7 @@
         out_specs=[vmem] * n_out,
         scratch_shapes=leaves,
         compiler_params=pltpu.CompilerParams(
-            collective_id=0, has_side_effects=True, vmem_limit_bytes=53 << 20
+            collective_id=0, has_side_effects=True, vmem_limit_bytes=48 << 20
         ),
         name="block",
     )(*(pltpu.with_memory_space_constraint(a, pltpu.HBM) for a in operands))

time: 77.1 us -> 68.8 us (0.89)
  local copies, waits for them, and re-layouts: 6.15 us -> 0 us
  Pallas kernels: 69.8 us -> 67.8 us
    unnamed x10 -> x0, local copies, waits for them, and re-layouts: 6.15 us -> none
    pallas_call x1, Pallas kernels: 67.1 us -> 65.2 us  [on_device(): pl.pallas_call(body, out_shape=results, in_specs=[hbm] * n_in, out_specs=...]
where the time goes in v4:
time: 68.8 us; the launch traced here: 68.7 us
  Pallas kernels  67.8 us (99%)
  between operations  0.82 us (1%)
    pallas_call x1, Pallas kernels, on_device(): pl.pallas_call(body, out_shape=results, in_specs=[hbm] * n_in, out_specs=...  65.2 us
    pallas_call x1, Pallas kernels, on_device(): pl.pallas_call(put_out, out_shape=results, in_specs=[vmem] * n_out, out_s...  2.68 us

profile of v4, /device:TPU:0, one launch (start us, length us, event | category | flops | bytes accessed | tf_op | source)
XLA Modules:
  0.0 68.7 jit_solution(1559328202512928154)
XLA Ops:
  0.6 65.2 %block.1 = (f32[197,2,384]{2,1,0:T(2,128)S(1)}, f32[197,2,384]{2,1,0:T(2,128)S(1)}, f32[384]{0:T(512)S(1)}, f32[384,1152]{1,0:T(8,128)S(1)}, f32[384,384]{1,0:T(...) custom-call(bf16[197,2,384]{2,1,0:T(2,128)(2,1)} %bitcast.10, ...), custom_call_target="tpu_custom_call" | custom-call | tf_op jit(solution)/shard_map/block/pallas_call | solution.py:972
  65.8 2.7 %put_out.1 = (f32[197,2,384]{2,1,0:T(2,128)}, f32[197,2,384]{2,1,0:T(2,128)}, f32[384]{0:T(512)}, f32[384,1152]{1,0:T(8,128)}, f32[384,384]{1,0:T(8,128)}, /*ind...) custom-call(f32[197,2,384]{2,1,0:T(2,128)S(1)} %get-tuple-element.27.refs_0_, ...), custom_call_target="tpu_custom_call" | custom-call | tf_op jit(solution)/shard_map/put_out/pallas_call | solution.py:995

commit v5 on v4

--- a/solution.py
+++ b/solution.py
@@ -17,7 +17,7 @@
 EPS = 1e-06
 TP = 208
 TL = 256
-SM = 32
+SM = 8
 ROWS = (256, 128, 128, 256, 256, 256, 256)
 START = (0, 256, 384, 512, 768, 1024, 1280)
 CHUNKS = ((0,), (1, 2), (3,), (4,), (5,), (6,))
@@ -775,16 +775,18 @@
         experts(mb, lambda: for_core(1, lambda: exchange(("back", mb - 1))))
         exchange(("ggrad", mb))
         exchange(("back", mb))
-        weight_grads(mb, (0,))
+        weight_grads(mb, (0, 1))
     swap_slices(0)
+    swap_slices(1)
     exchange(*(("made", mb) for mb in range(last)))
     small_ref[...] = jnp.zeros_like(small_ref)
+    sent_early = min(0, pieces)
     for mb in range(MB):
         backward(mb)
-
-    def late_slices():
-        weight_grads(last, (1,))
-        swap_slices(1)
+        if mb == last - 1:
+            add_slices(1)
+            for piece in range(sent_early):
+                hand_out((1, piece))
 
     def small_begin():
         t1_ref[r] = small_ref[...].astype(BF16)
@@ -803,20 +805,18 @@
         steps = (sum_first, sum_second, spread_first, spread_parts)
         plan.extend((when, step, ck) for when, step in zip(times, steps))
         plan.append((times[3] + 1.2, store_totals, ck))
-    for piece in range(pieces):
+    for piece in range(sent_early, pieces):
         plan.append((X_TIMES[piece % 4], hand_out, (1, piece)))
     plan.append((-0.15, finish, last))
-    plan.append((0.2, lambda _: late_slices(), 0))
     for mb in range(last):
         plan.append((0.5, finish, mb))
     plan.append((0.6, lambda _: small_begin(), 0))
     plan.append((0.5, lambda _: exchange(("made", last)), 0))
-    plan.append((4.9, add_slices, 1))
-    plan.append((3.0, combine, 0))
-    plan.append((2.7, small_next, 0))
+    plan.append((7.0, combine, 0))
+    plan.append((5.8, small_next, 0))
     for mb in range(1, MB):
         plan.append((10.0, combine, mb))
-    plan.append((6.0, small_next, 1))
+    plan.append((10.7, small_next, 1))
     plan.append((9.2, slices_out, 0))
     plan.append((17.0, slices_out, 1))
     plan.append((17.1, lambda _: small_end(), 0))

time: 68.8 us -> 67.3 us (0.978)
  Pallas kernels: 67.8 us -> 66.4 us
    pallas_call x1, Pallas kernels: 65.2 us -> 63.7 us  [on_device(): pl.pallas_call(body, out_shape=results, in_specs=[hbm] * n_in, out_specs=...]
where the time goes in v5:
time: 67.3 us; the launch traced here: 67.2 us
  Pallas kernels  66.4 us (99%)
  between operations  0.82 us (1%)
    pallas_call x1, Pallas kernels, on_device(): pl.pallas_call(body, out_shape=results, in_specs=[hbm] * n_in, out_specs=...  63.7 us
    pallas_call x1, Pallas kernels, on_device(): pl.pallas_call(put_out, out_shape=results, in_specs=[vmem] * n_out, out_s...  2.68 us

profile of v5, /device:TPU:0, one launch (start us, length us, event | category | flops | bytes accessed | tf_op | source)
XLA Modules:
  0.0 67.2 jit_solution(10460491865028932336)
XLA Ops:
  0.6 63.7 %block.1 = (f32[197,2,384]{2,1,0:T(2,128)S(1)}, f32[197,2,384]{2,1,0:T(2,128)S(1)}, f32[384]{0:T(512)S(1)}, f32[384,1152]{1,0:T(8,128)S(1)}, f32[384,384]{1,0:T(...) custom-call(bf16[197,2,384]{2,1,0:T(2,128)(2,1)} %bitcast.10, ...), custom_call_target="tpu_custom_call" | custom-call | tf_op jit(solution)/shard_map/block/pallas_call | solution.py:972
  64.3 2.7 %put_out.1 = (f32[197,2,384]{2,1,0:T(2,128)}, f32[197,2,384]{2,1,0:T(2,128)}, f32[384]{0:T(512)}, f32[384,1152]{1,0:T(8,128)}, f32[384,384]{1,0:T(8,128)}, /*ind...) custom-call(f32[197,2,384]{2,1,0:T(2,128)S(1)} %get-tuple-element.27.refs_0_, ...), custom_call_target="tpu_custom_call" | custom-call | tf_op jit(solution)/shard_map/put_out/pallas_call | solution.py:995

commit v6 on v5

--- a/solution.py
+++ b/solution.py
@@ -179,7 +179,7 @@
         for send, recv, sems in legs:
             pltpu.make_async_copy(send.at[me], recv.at[me], sems.at[1]).start()
 
-        @pl.loop(1, G)
+        @pl.loop(1, G, unroll=True)
         def _(o):
             e = (me + o) % G
             to = group_id(e)

time: 67.3 us -> 67.2 us (level)
  no operation moved by 1% of the time
where the time goes in v6:
time: 67.2 us; the launch traced here: 67.1 us
  Pallas kernels  66.2 us (99%)
  between operations  0.82 us (1%)
    pallas_call x1, Pallas kernels, on_device(): pl.pallas_call(body, out_shape=results, in_specs=[hbm] * n_in, out_specs=...  63.6 us
    pallas_call x1, Pallas kernels, on_device(): pl.pallas_call(put_out, out_shape=results, in_specs=[vmem] * n_out, out_s...  2.68 us

profile of v6, /device:TPU:0, one launch (start us, length us, event | category | flops | bytes accessed | tf_op | source)
XLA Modules:
  0.0 67.1 jit_solution(8330616691687187803)
XLA Ops:
  0.6 63.6 %block.1 = (f32[197,2,384]{2,1,0:T(2,128)S(1)}, f32[197,2,384]{2,1,0:T(2,128)S(1)}, f32[384]{0:T(512)S(1)}, f32[384,1152]{1,0:T(8,128)S(1)}, f32[384,384]{1,0:T(...) custom-call(bf16[197,2,384]{2,1,0:T(2,128)(2,1)} %bitcast.10, ...), custom_call_target="tpu_custom_call" | custom-call | tf_op jit(solution)/shard_map/block/pallas_call | solution.py:972
  64.2 2.7 %put_out.1 = (f32[197,2,384]{2,1,0:T(2,128)}, f32[197,2,384]{2,1,0:T(2,128)}, f32[384]{0:T(512)}, f32[384,1152]{1,0:T(8,128)}, f32[384,384]{1,0:T(8,128)}, /*ind...) custom-call(f32[197,2,384]{2,1,0:T(2,128)S(1)} %get-tuple-element.27.refs_0_, ...), custom_call_target="tpu_custom_call" | custom-call | tf_op jit(solution)/shard_map/put_out/pallas_call | solution.py:995
